TPU v7x, 256 devices: a whole 4x4x8 slice. The times are simulated.
256 devices in a mesh: obs: 8 (over x, core), ord: 32 (over y, z).
Axes of the slice: x: 4, y: 4, z: 8, core: 2. Of those that a mesh axis runs over, the one named last changes fastest.
Arguments:
- longitude: float32 [8, 32768], P('obs'), may hold values from -3.140625 to 3.140625
- cycle_of: int32 [8, 32768], P('obs'), may hold values from 0 to 255, never falling along the last dimension, each value on 1 to 256 neighbouring positions
- obs_count: int32 [8], P('obs'), may hold values from 16384 to 32768
- observed: float32 [8, 32768], P('obs'), may hold values from -1792 to 1792
- obs_weight: float32 [8, 32768], P('obs'), may hold values from 0.3 to 3
- legendre: float32 [8, 288, 288, 256], P('obs', 'ord'), as said below
- precond_inv: float32 [288, 288, 288], P('ord'), as said below
- order_of_slot: int32 [288], P('ord'), may hold values from 0 to 287, each once
Outputs:
- solution: float32 [288, 2, 288], P('ord')
- residual: float32 [288, 2, 288], P('ord')
Inputs may be any that keep to these rules, and one draw needn't show every extreme that they name: `cycle_of`: cycle numbers never fall along a slab; each cycle holds at least one observation slot. `obs_count`: observation slots at or beyond a slab's count carry no weight. legendre[b, m, n, j] is the fully normalized associated Legendre function of degree n and order m at the colatitude of cycle j of slab b, and 0 for n < m. `precond_inv`: every block is symmetric positive definite. order_of_slot names each order once; slot s lies on ord index s // 9.
All inputs are finite; a program needn't handle non-finite values.
Results may differ from a plain program's by a relative error of at most 0.0003.
Values sent between devices are 32-bit elements; how exact they have to be, the bound alone decides.
A program may use at most 128 MiB of HBM per device.

v0:
```python
import math

import jax
import jax.numpy as jnp
from jax import lax
from jax.sharding import PartitionSpec as P

ITERS = 2


PRECISE = lax.Precision.HIGHEST


def sent_to_all(array, axis):
    copies = jnp.broadcast_to(array, (lax.axis_size(axis), *array.shape))
    return lax.all_to_all(copies, axis, split_axis=0, concat_axis=0, tiled=True)


def laid_out(tiles, dim):
    tiles = jnp.moveaxis(tiles, 0, dim)
    shape = tiles.shape
    return tiles.reshape(*shape[:dim], shape[dim] * shape[dim + 1], *shape[dim + 2 :])


def collect(array, axis, dim):
    tiles = sent_to_all(array, axis)
    return laid_out(tiles, dim)


def in_blocks(array, dim, devices):
    shape = array.shape
    tiles = array.reshape(*shape[:dim], devices, shape[dim] // devices, *shape[dim + 1 :])
    return jnp.moveaxis(tiles, dim, 0)


def summed_on_arrival(array, axis, dim):
    devices = lax.axis_size(axis)
    tiles = lax.all_to_all(in_blocks(array, dim, devices), axis, 0, 0, tiled=True)
    return jnp.sum(tiles, axis=0)


def rows_for(lines, devices):
    spare = -lines.shape[0] % devices
    if not spare:
        return lines
    return jnp.concatenate([lines, jnp.zeros((spare, *lines.shape[1:]), lines.dtype)])


def sum_by_parts(array, axes):
    lines = array.reshape(-1)
    own = summed_on_arrival(rows_for(lines, lax.axis_size(axes)), axes, 0)
    whole = collect(own, axes, 0)
    return whole[: len(lines)].reshape(array.shape)


def taken_together(array, axis):
    return sent_to_all(array, axis).sum(axis=0)


def block_split(cycle_ids):
    slab_size = cycle_ids.shape[0]
    block = math.gcd(slab_size, 4096)
    return (block, slab_size // block)


def spread_cycles(cycle_values, cycle_ids):
    rows = cycle_values.shape[0] * cycle_values.shape[1]
    cycle_count = cycle_values.shape[2]
    flat_cycles = cycle_values.reshape(rows, cycle_count)
    block, blocks = block_split(cycle_ids)
    cycle_iota = jnp.arange(cycle_count, dtype=jnp.int32)

    def one_block(id_block):
        onehot = (id_block[:, None] == cycle_iota[None, :]).astype(jnp.float32)
        return jnp.dot(onehot, flat_cycles.T, precision=PRECISE, preferred_element_type=jnp.float32)

    pieces = lax.map(one_block, cycle_ids.reshape(blocks, block))
    at_points = pieces.reshape(blocks * block, rows).T
    return at_points.reshape(cycle_values.shape[0], cycle_values.shape[1], blocks * block)


def collect_cycles(weighted, cycle_ids, cycle_count):
    lead = weighted.shape[0]
    pair = weighted.shape[1]
    rows = lead * pair
    block, blocks = block_split(cycle_ids)
    cycle_iota = jnp.arange(cycle_count, dtype=jnp.int32)
    flat = jnp.moveaxis(weighted.reshape(rows, blocks, block), 1, 0)

    def add_block(total, block_data):
        id_block, value_block = block_data
        onehot = (id_block[:, None] == cycle_iota[None, :]).astype(jnp.float32)
        return (
            total
            + jnp.dot(value_block, onehot, precision=PRECISE, preferred_element_type=jnp.float32),
            None,
        )

    total, unused = lax.scan(
        add_block,
        jnp.zeros((rows, cycle_count), jnp.float32),
        (cycle_ids.reshape(blocks, block), flat),
    )
    return total.reshape(lead, pair, cycle_count)


def synthesize(coefficients, legendre_here, harmonic, cycle_ids):
    cycle_values = jnp.einsum("okn,onr->okr", coefficients, legendre_here, precision=PRECISE)
    at_points = spread_cycles(cycle_values, cycle_ids)
    return jnp.sum(at_points * harmonic, axis=(0, 1))


def adjoint(values, legendre_here, harmonic, cycle_ids):
    weighted = harmonic * values[None, None, :]
    per_cycle = collect_cycles(weighted, cycle_ids, legendre_here.shape[2])
    return jnp.einsum("okr,onr->okn", per_cycle, legendre_here, precision=PRECISE)


def body(
    longitude, cycle_of, obs_count, observed, obs_weight, legendre, precond_inv, order_of_slot
):
    count_here = legendre.shape[1]
    degrees = legendre.shape[2]
    legendre_here = legendre[0]
    east = longitude[0]
    cycle_ids = cycle_of[0]
    slab_size = east.shape[0]
    positions = jnp.arange(slab_size, dtype=jnp.int32)
    total_obs = slab_size * lax.axis_size("obs")
    obs_scale = obs_weight[0] * (positions < obs_count[0]).astype(jnp.float32) / total_obs
    first_order = lax.axis_index("ord") * count_here
    block_orders = first_order + jnp.arange(count_here, dtype=jnp.int32)
    angles = block_orders.astype(jnp.float32)[:, None] * east[None, :]
    harmonic = jnp.stack([jnp.cos(angles), jnp.sin(angles)], axis=1)
    every_owner = collect(order_of_slot, "ord", 0)
    slot_ids = jnp.arange(every_owner.shape[0], dtype=jnp.int32)
    slot_of_block = jnp.sum(
        jnp.where(every_owner[None, :] == block_orders[:, None], slot_ids[None, :], 0), axis=1
    )
    live_mask = (
        jnp.arange(degrees, dtype=jnp.int32)[None, None, :] >= order_of_slot[:, None, None]
    ).astype(jnp.float32)
    share_width = degrees // lax.axis_size("obs")
    share_start = lax.axis_index("obs") * share_width

    def owner_rows(partial_value):
        degree_piece = summed_on_arrival(partial_value, "obs", 2)
        everyone = collect(degree_piece, "ord", 0)
        owned_rows = jnp.take(everyone, order_of_slot, axis=0)
        return collect(owned_rows, "obs", 2)

    def precondition(values):
        return live_mask * jnp.einsum("snj,skj->skn", precond_inv, values, precision=PRECISE)

    def energy(values, precond):
        return taken_together(jnp.sum(values * precond), "ord")

    residual = owner_rows(adjoint(obs_scale * observed[0], legendre_here, harmonic, cycle_ids))
    solution = jnp.zeros_like(residual)
    precond = precondition(residual)
    direction = precond
    energy_now = energy(residual, precond)
    for iteration in range(ITERS):
        block_degree_piece = lax.dynamic_slice_in_dim(direction, share_start, share_width, 2)
        block_everyone = collect(block_degree_piece, "ord", 0)
        block_piece = jnp.take(block_everyone, slot_of_block, axis=0)
        coefficients = collect(block_piece, "obs", 2)
        gradient = sum_by_parts(synthesize(coefficients, legendre_here, harmonic, cycle_ids), "ord")
        weighted = obs_scale * gradient
        curvature_sum = taken_together(jnp.sum(weighted * gradient), "obs")
        image = owner_rows(adjoint(weighted, legendre_here, harmonic, cycle_ids))
        image, curvature_sum = (image, curvature_sum)
        step_size = energy_now / curvature_sum
        solution = solution + step_size * direction
        residual = residual - step_size * image
        if iteration + 1 < ITERS:
            precond = precondition(residual)
            energy_next = energy(residual, precond)
            direction = precond + energy_next / energy_now * direction
            energy_now = energy_next
    return (solution, residual)


def solution(mesh):
    placed = (
        P("obs", None),
        P("obs", None),
        P("obs"),
        P("obs", None),
        P("obs", None),
        P("obs", "ord", None, None),
        P("ord", None, None),
        P("ord"),
    )
    return jax.shard_map(
        body,
        mesh=mesh,
        in_specs=placed,
        out_specs=(P("ord", None, None), P("ord", None, None)),
        check_vma=False,
    )
```

profile of v0, /device:TPU:1, one launch (start us, length us, event | category | flops | bytes accessed | tf_op | source)
XLA Modules:
  0.0 623.7 jit_solution(10238624991343988768)
XLA Ops:
  0.7 34.1 %multiply_cosine_fusion = (f32[9,1,32768]{2,1,0:T(1,128)S(1)}, f32[9,1,32768]{2,1,0:T(1,128)S(1)}) fusion(f32[32768]{0:T(1024)} %bitcast.158, f32[9]{0:T(128)S(1)} %fusion.39), kind=kLoop, calls=%fused_computation.58 | loop fusion | flops 294912 | bytes 2490404 | tf_op jit(solution)/shard_map/cos | solution.py:134
  50.6 28.7 %while.57 = (s32[]{:T(128)}, f32[18,256]{1,0:T(8,128)S(1)}, f32[8,18,4096]{2,0,1:T(8,128)}, s32[8,4096]{1,0:T(8,128)S(1)}, s32[]{:T(128)}, /*index=5*/s32[]{:T(128)}) while((s32[]{:T(128)}, f32[18,256]{1,0:T(8,128)S(1)}, f32[8,18,4096]{2,0,1:T(8,128)}, s32[8,4096]{1,0:T(8,128)S(1)}, s32[]{:T(128)}, /*index=5*/s32[]{:T(128)}) %tuple.108), condition=%wide.region_1.2_spmd.clone, body=%wide.region_0.1_spmd.clone.sunk | while | flops 227550208 | bytes 970839 | solution.py:99
  82.5 6.4 %all-to-all-start = ((f32[8,1,648]{2,1,0:T(1,128)}), f32[8,1,648]{2,1,0:T(1,128)S(1)}, u32[]{:S(2)}, u32[]{:S(2)}) async-start(f32[8,1,648]{2,1,0:T(1,128)} %reshape.412), calls=%async_computation | async-start | bytes 49152 | tf_op jit(solution)/shard_map/all_to_all | solution.py:38
  94.3 10.5 %all-to-all-start.5 = ((s32[32,1,9]{2,1,0:T(1,128)}), s32[32,1,9]{2,1,0:T(1,128)S(1)}, u32[]{:S(2)}, u32[]{:S(2)}) async-start(s32[32,1,9]{2,1,0:T(1,128)} %broadcast_in_dim.101), calls=%async_computation.5 | async-start | bytes 32768 | tf_op jit(solution)/shard_map/all_to_all | solution.py:16
  107.2 6.2 all-to-all-done.5
  118.2 8.0 %all-to-all-done.1 = f32[32,1,648]{2,1,0:T(1,128)S(1)} async-done(((f32[32,1,648]{2,1,0:T(1,128)}), f32[32,1,648]{2,1,0:T(1,128)S(1)}, u32[]{:S(2)}, u32[]{:S(2)}) %all-to-all-start.1) | async-done | bytes 82976 | tf_op jit(solution)/shard_map/all_to_all | solution.py:16
  128.8 6.5 %all-to-all-start.2 = ((f32[8,1,648]{2,1,0:T(1,128)}), f32[8,1,648]{2,1,0:T(1,128)S(1)}, u32[]{:S(2)}, u32[]{:S(2)}) async-start(f32[8,1,648]{2,1,0:T(1,128)} %reshape.416), calls=%async_computation.2 | async-start | bytes 49152 | tf_op jit(solution)/shard_map/all_to_all | solution.py:16
  135.3 4.7 all-to-all-done.2
  140.9 6.3 %multiply_reduce_fusion.1 = (f32[]{:T(128)}, f32[9,2,288]{2,1,0:T(2,128)S(1)}) fusion(f32[9,2,288]{2,1,0:T(2,128)S(1)} %reshape.303, f32[9,288,288]{2,1,0:T(8,128)} %param.26, f32[9,288]{1,0:T(8,128)} %fusion.38), kind=kOutput, calls=%fused_computation.80 | convolution fusion | flops 17931456 | bytes 3037828 | tf_op jit(solution)/shard_map/snj,skj->skn/dot_general | solution.py:153
  152.2 9.0 %all-to-all-done.4 = f32[32,1,648]{2,1,0:T(1,128)S(1)} async-done(((f32[32,1,648]{2,1,0:T(1,128)}), f32[32,1,648]{2,1,0:T(1,128)S(1)}, u32[]{:S(2)}, u32[]{:S(2)}) %all-to-all-start.4) | async-done | bytes 82976 | tf_op jit(solution)/shard_map/all_to_all | solution.py:16
  163.7 5.3 all-to-all-start.6
  169.0 4.5 stack.11
  177.6 75.7 %while.55 = (s32[]{:T(128)}, f32[8,4096,18]{1,0,2:T(8,128)}, s32[8,4096]{1,0:T(8,128)S(1)}, f32[18,256]{1,0:T(8,128)S(1)}, s32[]{:T(128)}, /*index=5*/s32[]{:T(128)}) while((s32[]{:T(128)}, f32[8,4096,18]{1,0,2:T(8,128)}, s32[8,4096]{1,0:T(8,128)S(1)}, f32[18,256]{1,0:T(8,128)S(1)}, s32[]{:T(128)}, /*index=5*/s32[]{:T(128)}) %tuple.123), condition=%wide.region_7.9_spmd.clone, body=%wide.region_6.8_spmd.clone.sunk | while | flops 227540992 | bytes 1542221 | solution.py:77
  180.5 6.6 %dynamic_update_slice.11 = f32[8,4096,18]{1,0,2:T(8,128)} dynamic-update-slice(f32[8,4096,18]{1,0,2:T(8,128)} %get-tuple-element.458, f32[1,4096,18]{1,0,2:T(1,128)S(1)} %copy.111, s32[]{:T(128)} %get-tuple-element.457, s32[]{:T(128)} %constant.69.clone.1..sunk, s32[]{:T(128)} %constant.69.clone.1..sunk) | dynamic-update-slice | bytes 589828 | tf_op jit(solution)/shard_map/while/body/jit(dynamic_update_index_in_dim)/dynamic_update_slice | solution.py:77
  189.9 6.6 %dynamic_update_slice.11 = f32[8,4096,18]{1,0,2:T(8,128)} dynamic-update-slice(f32[8,4096,18]{1,0,2:T(8,128)} %get-tuple-element.458, f32[1,4096,18]{1,0,2:T(1,128)S(1)} %copy.111, s32[]{:T(128)} %get-tuple-element.457, s32[]{:T(128)} %constant.69.clone.1..sunk, s32[]{:T(128)} %constant.69.clone.1..sunk) | dynamic-update-slice | bytes 589828 | tf_op jit(solution)/shard_map/while/body/jit(dynamic_update_index_in_dim)/dynamic_update_slice | solution.py:77
  199.4 6.6 %dynamic_update_slice.11 = f32[8,4096,18]{1,0,2:T(8,128)} dynamic-update-slice(f32[8,4096,18]{1,0,2:T(8,128)} %get-tuple-element.458, f32[1,4096,18]{1,0,2:T(1,128)S(1)} %copy.111, s32[]{:T(128)} %get-tuple-element.457, s32[]{:T(128)} %constant.69.clone.1..sunk, s32[]{:T(128)} %constant.69.clone.1..sunk) | dynamic-update-slice | bytes 589828 | tf_op jit(solution)/shard_map/while/body/jit(dynamic_update_index_in_dim)/dynamic_update_slice | solution.py:77
  208.9 6.6 %dynamic_update_slice.11 = f32[8,4096,18]{1,0,2:T(8,128)} dynamic-update-slice(f32[8,4096,18]{1,0,2:T(8,128)} %get-tuple-element.458, f32[1,4096,18]{1,0,2:T(1,128)S(1)} %copy.111, s32[]{:T(128)} %get-tuple-element.457, s32[]{:T(128)} %constant.69.clone.1..sunk, s32[]{:T(128)} %constant.69.clone.1..sunk) | dynamic-update-slice | bytes 589828 | tf_op jit(solution)/shard_map/while/body/jit(dynamic_update_index_in_dim)/dynamic_update_slice | solution.py:77
  218.3 6.6 %dynamic_update_slice.11 = f32[8,4096,18]{1,0,2:T(8,128)} dynamic-update-slice(f32[8,4096,18]{1,0,2:T(8,128)} %get-tuple-element.458, f32[1,4096,18]{1,0,2:T(1,128)S(1)} %copy.111, s32[]{:T(128)} %get-tuple-element.457, s32[]{:T(128)} %constant.69.clone.1..sunk, s32[]{:T(128)} %constant.69.clone.1..sunk) | dynamic-update-slice | bytes 589828 | tf_op jit(solution)/shard_map/while/body/jit(dynamic_update_index_in_dim)/dynamic_update_slice | solution.py:77
  227.8 6.6 %dynamic_update_slice.11 = f32[8,4096,18]{1,0,2:T(8,128)} dynamic-update-slice(f32[8,4096,18]{1,0,2:T(8,128)} %get-tuple-element.458, f32[1,4096,18]{1,0,2:T(1,128)S(1)} %copy.111, s32[]{:T(128)} %get-tuple-element.457, s32[]{:T(128)} %constant.69.clone.1..sunk, s32[]{:T(128)} %constant.69.clone.1..sunk) | dynamic-update-slice | bytes 589828 | tf_op jit(solution)/shard_map/while/body/jit(dynamic_update_index_in_dim)/dynamic_update_slice | solution.py:77
  237.3 6.6 %dynamic_update_slice.11 = f32[8,4096,18]{1,0,2:T(8,128)} dynamic-update-slice(f32[8,4096,18]{1,0,2:T(8,128)} %get-tuple-element.458, f32[1,4096,18]{1,0,2:T(1,128)S(1)} %copy.111, s32[]{:T(128)} %get-tuple-element.457, s32[]{:T(128)} %constant.69.clone.1..sunk, s32[]{:T(128)} %constant.69.clone.1..sunk) | dynamic-update-slice | bytes 589828 | tf_op jit(solution)/shard_map/while/body/jit(dynamic_update_index_in_dim)/dynamic_update_slice | solution.py:77
  246.7 6.6 %dynamic_update_slice.11 = f32[8,4096,18]{1,0,2:T(8,128)} dynamic-update-slice(f32[8,4096,18]{1,0,2:T(8,128)} %get-tuple-element.458, f32[1,4096,18]{1,0,2:T(1,128)S(1)} %copy.111, s32[]{:T(128)} %get-tuple-element.457, s32[]{:T(128)} %constant.69.clone.1..sunk, s32[]{:T(128)} %constant.69.clone.1..sunk) | dynamic-update-slice | bytes 589828 | tf_op jit(solution)/shard_map/while/body/jit(dynamic_update_index_in_dim)/dynamic_update_slice | solution.py:77
  257.8 12.2 %all_to_all.133 = f32[32,1,1024]{2,1,0:T(1,128)S(1)} all-to-all(f32[32,1,1024]{2,1,0:T(1,128)S(1)} %bitcast.140), channel_id=1, replica_groups=mesh['obs'=8,'ord'=32] {'ord'}, dimensions={0} | all-to-all | bytes 262144 | tf_op jit(solution)/shard_map/all_to_all | solution.py:38
  274.7 9.1 %all-to-all-done.8 = f32[32,1,1024]{2,1,0:T(1,128)S(1)} async-done(((f32[32,1,1024]{2,1,0:T(1,128)}), f32[32,1,1024]{2,1,0:T(1,128)S(1)}, u32[]{:S(2)}, u32[]{:S(2)}) %all-to-all-start.8) | async-done | bytes 131104 | tf_op jit(solution)/shard_map/all_to_all | solution.py:16
  287.6 28.2 %while.58 = (s32[]{:T(128)}, f32[18,256]{1,0:T(8,128)S(1)}, f32[8,18,4096]{2,0,1:T(8,128)}, s32[8,4096]{1,0:T(8,128)S(1)}, s32[]{:T(128)}, /*index=5*/s32[]{:T(128)}) while((s32[]{:T(128)}, f32[18,256]{1,0:T(8,128)S(1)}, f32[8,18,4096]{2,0,1:T(8,128)}, s32[8,4096]{1,0:T(8,128)S(1)}, s32[]{:T(128)}, /*index=5*/s32[]{:T(128)}) %tuple.124), condition=%wide.region_13.15_spmd.clone, body=%wide.region_12.14_spmd.clone.sunk | while | flops 227550208 | bytes 970839 | solution.py:99
  318.4 12.4 %all_to_all.134 = f32[8,1,648]{2,1,0:T(1,128)S(1)} all-to-all(f32[8,1,648]{2,1,0:T(1,128)S(1)} %reshape.422), channel_id=1, replica_groups=mesh['obs'=8,'ord'=32] {'obs'}, dimensions={0} | all-to-all | bytes 41472 | tf_op jit(solution)/shard_map/all_to_all | solution.py:38
  338.2 7.5 %all-to-all-done.11 = f32[32,1,648]{2,1,0:T(1,128)S(1)} async-done(((f32[32,1,648]{2,1,0:T(1,128)}), f32[32,1,648]{2,1,0:T(1,128)S(1)}, u32[]{:S(2)}, u32[]{:S(2)}) %all-to-all-start.11) | async-done | bytes 82976 | tf_op jit(solution)/shard_map/all_to_all | solution.py:16
  354.9 4.5 all-to-all-done.3
  360.0 10.0 %all_to_all.131 = f32[8,1,1]{2,1,0:T(1,128)S(1)} all-to-all(f32[8,1,1]{2,1,0:T(1,128)S(1)} %broadcast_in_dim.106), channel_id=1, replica_groups=mesh['obs'=8,'ord'=32] {'obs'}, dimensions={0} | all-to-all | bytes 64 | tf_op jit(solution)/shard_map/all_to_all | solution.py:16
  380.3 6.2 multiply_reduce_fusion
  387.1 12.3 %all_to_all.135 = f32[32,1,1]{2,1,0:T(1,128)S(1)} all-to-all(f32[32,1,1]{2,1,0:T(1,128)S(1)} %broadcast_in_dim.109), channel_id=1, replica_groups=mesh['obs'=8,'ord'=32] {'ord'}, dimensions={0} | all-to-all | bytes 256 | tf_op jit(solution)/shard_map/all_to_all | solution.py:16
  402.6 12.0 %all_to_all.132 = f32[32,1,648]{2,1,0:T(1,128)S(1)} all-to-all(f32[32,1,648]{2,1,0:T(1,128)S(1)} %reshape.428), channel_id=1, replica_groups=mesh['obs'=8,'ord'=32] {'ord'}, dimensions={0} | all-to-all | bytes 165888 | tf_op jit(solution)/shard_map/all_to_all | solution.py:16
  418.7 6.8 %all-to-all-start.15 = ((f32[8,1,648]{2,1,0:T(1,128)}), f32[8,1,648]{2,1,0:T(1,128)S(1)}, u32[]{:S(2)}, u32[]{:S(2)}) async-start(f32[8,1,648]{2,1,0:T(1,128)} %reshape.430), calls=%async_computation.15 | async-start | bytes 49152 | tf_op jit(solution)/shard_map/all_to_all | solution.py:16
  425.6 4.7 all-to-all-done.15
  434.2 75.7 %while.56 = (s32[]{:T(128)}, f32[8,4096,18]{1,0,2:T(8,128)}, s32[8,4096]{1,0:T(8,128)S(1)}, f32[18,256]{1,0:T(8,128)S(1)}, s32[]{:T(128)}, /*index=5*/s32[]{:T(128)}) while((s32[]{:T(128)}, f32[8,4096,18]{1,0,2:T(8,128)}, s32[8,4096]{1,0:T(8,128)S(1)}, f32[18,256]{1,0:T(8,128)S(1)}, s32[]{:T(128)}, /*index=5*/s32[]{:T(128)}) %tuple.125), condition=%wide.region_18.20_spmd.clone, body=%wide.region_17.19_spmd.clone.sunk | while | flops 227540992 | bytes 1542221 | solution.py:77
  437.1 6.6 %dynamic_update_slice.12 = f32[8,4096,18]{1,0,2:T(8,128)} dynamic-update-slice(f32[8,4096,18]{1,0,2:T(8,128)} %get-tuple-element.494, f32[1,4096,18]{1,0,2:T(1,128)S(1)} %copy.112, s32[]{:T(128)} %get-tuple-element.493, s32[]{:T(128)} %constant.69.clone.1..sunk.1, s32[]{:T(128)} %constant.69.clone.1..sunk.1) | dynamic-update-slice | bytes 589828 | tf_op jit(solution)/shard_map/while/body/jit(dynamic_update_index_in_dim)/dynamic_update_slice | solution.py:77
  446.5 6.6 %dynamic_update_slice.12 = f32[8,4096,18]{1,0,2:T(8,128)} dynamic-update-slice(f32[8,4096,18]{1,0,2:T(8,128)} %get-tuple-element.494, f32[1,4096,18]{1,0,2:T(1,128)S(1)} %copy.112, s32[]{:T(128)} %get-tuple-element.493, s32[]{:T(128)} %constant.69.clone.1..sunk.1, s32[]{:T(128)} %constant.69.clone.1..sunk.1) | dynamic-update-slice | bytes 589828 | tf_op jit(solution)/shard_map/while/body/jit(dynamic_update_index_in_dim)/dynamic_update_slice | solution.py:77
  456.0 6.6 %dynamic_update_slice.12 = f32[8,4096,18]{1,0,2:T(8,128)} dynamic-update-slice(f32[8,4096,18]{1,0,2:T(8,128)} %get-tuple-element.494, f32[1,4096,18]{1,0,2:T(1,128)S(1)} %copy.112, s32[]{:T(128)} %get-tuple-element.493, s32[]{:T(128)} %constant.69.clone.1..sunk.1, s32[]{:T(128)} %constant.69.clone.1..sunk.1) | dynamic-update-slice | bytes 589828 | tf_op jit(solution)/shard_map/while/body/jit(dynamic_update_index_in_dim)/dynamic_update_slice | solution.py:77
  465.5 6.6 %dynamic_update_slice.12 = f32[8,4096,18]{1,0,2:T(8,128)} dynamic-update-slice(f32[8,4096,18]{1,0,2:T(8,128)} %get-tuple-element.494, f32[1,4096,18]{1,0,2:T(1,128)S(1)} %copy.112, s32[]{:T(128)} %get-tuple-element.493, s32[]{:T(128)} %constant.69.clone.1..sunk.1, s32[]{:T(128)} %constant.69.clone.1..sunk.1) | dynamic-update-slice | bytes 589828 | tf_op jit(solution)/shard_map/while/body/jit(dynamic_update_index_in_dim)/dynamic_update_slice | solution.py:77
  474.9 6.6 %dynamic_update_slice.12 = f32[8,4096,18]{1,0,2:T(8,128)} dynamic-update-slice(f32[8,4096,18]{1,0,2:T(8,128)} %get-tuple-element.494, f32[1,4096,18]{1,0,2:T(1,128)S(1)} %copy.112, s32[]{:T(128)} %get-tuple-element.493, s32[]{:T(128)} %constant.69.clone.1..sunk.1, s32[]{:T(128)} %constant.69.clone.1..sunk.1) | dynamic-update-slice | bytes 589828 | tf_op jit(solution)/shard_map/while/body/jit(dynamic_update_index_in_dim)/dynamic_update_slice | solution.py:77
  484.4 6.6 %dynamic_update_slice.12 = f32[8,4096,18]{1,0,2:T(8,128)} dynamic-update-slice(f32[8,4096,18]{1,0,2:T(8,128)} %get-tuple-element.494, f32[1,4096,18]{1,0,2:T(1,128)S(1)} %copy.112, s32[]{:T(128)} %get-tuple-element.493, s32[]{:T(128)} %constant.69.clone.1..sunk.1, s32[]{:T(128)} %constant.69.clone.1..sunk.1) | dynamic-update-slice | bytes 589828 | tf_op jit(solution)/shard_map/while/body/jit(dynamic_update_index_in_dim)/dynamic_update_slice | solution.py:77
  493.9 6.6 %dynamic_update_slice.12 = f32[8,4096,18]{1,0,2:T(8,128)} dynamic-update-slice(f32[8,4096,18]{1,0,2:T(8,128)} %get-tuple-element.494, f32[1,4096,18]{1,0,2:T(1,128)S(1)} %copy.112, s32[]{:T(128)} %get-tuple-element.493, s32[]{:T(128)} %constant.69.clone.1..sunk.1, s32[]{:T(128)} %constant.69.clone.1..sunk.1) | dynamic-update-slice | bytes 589828 | tf_op jit(solution)/shard_map/while/body/jit(dynamic_update_index_in_dim)/dynamic_update_slice | solution.py:77
  503.3 6.6 %dynamic_update_slice.12 = f32[8,4096,18]{1,0,2:T(8,128)} dynamic-update-slice(f32[8,4096,18]{1,0,2:T(8,128)} %get-tuple-element.494, f32[1,4096,18]{1,0,2:T(1,128)S(1)} %copy.112, s32[]{:T(128)} %get-tuple-element.493, s32[]{:T(128)} %constant.69.clone.1..sunk.1, s32[]{:T(128)} %constant.69.clone.1..sunk.1) | dynamic-update-slice | bytes 589828 | tf_op jit(solution)/shard_map/while/body/jit(dynamic_update_index_in_dim)/dynamic_update_slice | solution.py:77
  514.4 12.2 %all_to_all.136 = f32[32,1,1024]{2,1,0:T(1,128)S(1)} all-to-all(f32[32,1,1024]{2,1,0:T(1,128)S(1)} %bitcast.139), channel_id=1, replica_groups=mesh['obs'=8,'ord'=32] {'ord'}, dimensions={0} | all-to-all | bytes 262144 | tf_op jit(solution)/shard_map/all_to_all | solution.py:38
  531.3 9.1 %all-to-all-done.17 = f32[32,1,1024]{2,1,0:T(1,128)S(1)} async-done(((f32[32,1,1024]{2,1,0:T(1,128)}), f32[32,1,1024]{2,1,0:T(1,128)S(1)}, u32[]{:S(2)}, u32[]{:S(2)}) %all-to-all-start.17) | async-done | bytes 131104 | tf_op jit(solution)/shard_map/all_to_all | solution.py:16
  544.2 28.2 %while.59 = (s32[]{:T(128)}, f32[18,256]{1,0:T(8,128)S(1)}, f32[8,18,4096]{2,0,1:T(8,128)}, s32[8,4096]{1,0:T(8,128)S(1)}, s32[]{:T(128)}, /*index=5*/s32[]{:T(128)}) while((s32[]{:T(128)}, f32[18,256]{1,0:T(8,128)S(1)}, f32[8,18,4096]{2,0,1:T(8,128)}, s32[8,4096]{1,0:T(8,128)S(1)}, s32[]{:T(128)}, /*index=5*/s32[]{:T(128)}) %tuple.126), condition=%wide.region_24.26_spmd.clone, body=%wide.region_23.25_spmd.clone.sunk | while | flops 227550208 | bytes 970839 | solution.py:99
  575.6 6.6 %all-to-all-start.19 = ((f32[8,1,648]{2,1,0:T(1,128)}), f32[8,1,648]{2,1,0:T(1,128)S(1)}, u32[]{:S(2)}, u32[]{:S(2)}) async-start(f32[8,1,648]{2,1,0:T(1,128)} %reshape.432), calls=%async_computation.19 | async-start | bytes 49152 | tf_op jit(solution)/shard_map/all_to_all | solution.py:38
  602.5 7.1 %all-to-all-done.20 = f32[32,1,648]{2,1,0:T(1,128)S(1)} async-done(((f32[32,1,648]{2,1,0:T(1,128)}), f32[32,1,648]{2,1,0:T(1,128)S(1)}, u32[]{:S(2)}, u32[]{:S(2)}) %all-to-all-start.20) | async-done | bytes 82976 | tf_op jit(solution)/shard_map/all_to_all | solution.py:16
  612.1 5.0 all-to-all-start.21
  (315 shorter events, 271.0 us)
Async XLA Ops:
  0.6 78.7 %copy-start = (f32[1,9,288,256]{3,2,1,0:T(8,128)S(1)}, f32[1,9,288,256]{3,2,1,0:T(8,128)}, u32[]{:S(2)}) copy-start(f32[1,9,288,256]{3,2,1,0:T(8,128)} %param.25) | copy-start | bytes 7962628
  38.3 5.5 copy-start.3
  38.3 6.4 %copy-start.9 = (f32[1,32768]{1,0:T(1,128)S(1)}, f32[1,32768]{1,0:T(1,128)}, u32[]{:S(2)}) copy-start(f32[1,32768]{1,0:T(1,128)} %param.23) | copy-start | bytes 393220
  38.3 8.0 %copy-start.10 = (s32[1,32768]{1,0:T(1,128)S(1)}, s32[1,32768]{1,0:T(1,128)}, u32[]{:S(2)}) copy-start(s32[1,32768]{1,0:T(1,128)} %param.21) | copy-start | bytes 393220
  79.3 9.7 %copy-start.11 = (s32[9]{0:T(128)S(1)}, s32[9]{0:T(128)}, u32[]{:S(2)}) copy-start(s32[9]{0:T(128)} %param.27) | copy-start | bytes 112
  82.5 11.1 %all-to-all-start = ((f32[8,1,648]{2,1,0:T(1,128)}), f32[8,1,648]{2,1,0:T(1,128)S(1)}, u32[]{:S(2)}, u32[]{:S(2)}) async-start(f32[8,1,648]{2,1,0:T(1,128)} %reshape.412), calls=%async_computation | async-start | bytes 49152 | tf_op jit(solution)/shard_map/all_to_all | solution.py:38
  94.3 19.1 %all-to-all-start.5 = ((s32[32,1,9]{2,1,0:T(1,128)}), s32[32,1,9]{2,1,0:T(1,128)S(1)}, u32[]{:S(2)}, u32[]{:S(2)}) async-start(s32[32,1,9]{2,1,0:T(1,128)} %broadcast_in_dim.101), calls=%async_computation.5 | async-start | bytes 32768 | tf_op jit(solution)/shard_map/all_to_all | solution.py:16
  113.4 12.9 %all-to-all-start.1 = ((f32[32,1,648]{2,1,0:T(1,128)}), f32[32,1,648]{2,1,0:T(1,128)S(1)}, u32[]{:S(2)}, u32[]{:S(2)}) async-start(f32[32,1,648]{2,1,0:T(1,128)} %reshape.414), calls=%async_computation.1 | async-start | bytes 196608 | tf_op jit(solution)/shard_map/all_to_all | solution.py:16
  128.8 11.2 %all-to-all-start.2 = ((f32[8,1,648]{2,1,0:T(1,128)}), f32[8,1,648]{2,1,0:T(1,128)S(1)}, u32[]{:S(2)}, u32[]{:S(2)}) async-start(f32[8,1,648]{2,1,0:T(1,128)} %reshape.416), calls=%async_computation.2 | async-start | bytes 49152 | tf_op jit(solution)/shard_map/all_to_all | solution.py:16
  140.9 6.3 %copy-start.4 = (f32[9,2,288]{2,1,0:T(2,128)}, f32[9,2,288]{2,1,0:T(2,128)S(1)}, u32[]{:S(2)}) copy-start(f32[9,2,288]{2,1,0:T(2,128)S(1)} %reshape.303) | copy-start | bytes 62212
  148.3 12.9 %all-to-all-start.4 = ((f32[32,1,648]{2,1,0:T(1,128)}), f32[32,1,648]{2,1,0:T(1,128)S(1)}, u32[]{:S(2)}, u32[]{:S(2)}) async-start(f32[32,1,648]{2,1,0:T(1,128)} %reshape.418), calls=%async_computation.4 | async-start | bytes 196608 | tf_op jit(solution)/shard_map/all_to_all | solution.py:16
  163.7 9.9 %all-to-all-start.6 = ((f32[8,1,648]{2,1,0:T(1,128)}), f32[8,1,648]{2,1,0:T(1,128)S(1)}, u32[]{:S(2)}, u32[]{:S(2)}) async-start(f32[8,1,648]{2,1,0:T(1,128)} %reshape.420), calls=%async_computation.6 | async-start | bytes 49152 | tf_op jit(solution)/shard_map/all_to_all | solution.py:16
  255.3 1.9 copy-start.1
  270.9 13.0 %all-to-all-start.8 = ((f32[32,1,1024]{2,1,0:T(1,128)}), f32[32,1,1024]{2,1,0:T(1,128)S(1)}, u32[]{:S(2)}, u32[]{:S(2)}) async-start(f32[32,1,1024]{2,1,0:T(1,128)} %broadcast_in_dim.105), calls=%async_computation.8 | async-start | bytes 262144 | tf_op jit(solution)/shard_map/all_to_all | solution.py:16
  332.7 12.9 %all-to-all-start.11 = ((f32[32,1,648]{2,1,0:T(1,128)}), f32[32,1,648]{2,1,0:T(1,128)S(1)}, u32[]{:S(2)}, u32[]{:S(2)}) async-start(f32[32,1,648]{2,1,0:T(1,128)} %reshape.424), calls=%async_computation.11 | async-start | bytes 196608 | tf_op jit(solution)/shard_map/all_to_all | solution.py:16
  346.9 12.5 %all-to-all-start.3 = ((f32[32,1,1]{2,1,0:T(1,128)}), f32[32,1,1]{2,1,0:T(1,128)S(1)}, u32[]{:S(2)}, u32[]{:S(2)}) async-start(f32[32,1,1]{2,1,0:T(1,128)} %broadcast_in_dim.99), calls=%async_computation.3 | async-start | bytes 32768 | tf_op jit(solution)/shard_map/all_to_all | solution.py:16
  369.9 8.6 %all-to-all-start.12 = ((f32[8,1,648]{2,1,0:T(1,128)}), f32[8,1,648]{2,1,0:T(1,128)S(1)}, u32[]{:S(2)}, u32[]{:S(2)}) async-start(f32[8,1,648]{2,1,0:T(1,128)} %reshape.426), calls=%async_computation.12 | async-start | bytes 49152 | tf_op jit(solution)/shard_map/all_to_all | solution.py:16
  380.2 21.4 %copy-start.5 = (f32[9,2,288]{2,1,0:T(2,128)}, f32[9,2,288]{2,1,0:T(2,128)S(1)}, u32[]{:S(2)}) copy-start(f32[9,2,288]{2,1,0:T(2,128)S(1)} %sub.6) | copy-start | bytes 62212
  401.5 0.6 copy-start.7
  418.7 11.5 %all-to-all-start.15 = ((f32[8,1,648]{2,1,0:T(1,128)}), f32[8,1,648]{2,1,0:T(1,128)S(1)}, u32[]{:S(2)}, u32[]{:S(2)}) async-start(f32[8,1,648]{2,1,0:T(1,128)} %reshape.430), calls=%async_computation.15 | async-start | bytes 49152 | tf_op jit(solution)/shard_map/all_to_all | solution.py:16
  511.9 1.9 copy-start.2
  527.4 13.0 %all-to-all-start.17 = ((f32[32,1,1024]{2,1,0:T(1,128)}), f32[32,1,1024]{2,1,0:T(1,128)S(1)}, u32[]{:S(2)}, u32[]{:S(2)}) async-start(f32[32,1,1024]{2,1,0:T(1,128)} %broadcast_in_dim.112), calls=%async_computation.17 | async-start | bytes 262144 | tf_op jit(solution)/shard_map/all_to_all | solution.py:16
  572.4 44.7 %copy-start.8 = (f32[9,2,288]{2,1,0:T(2,128)S(1)}, f32[9,2,288]{2,1,0:T(2,128)}, u32[]{:S(2)}) copy-start(f32[9,2,288]{2,1,0:T(2,128)} %copy-done.7) | copy-start | bytes 62212
  572.4 50.2 %copy-start.6 = (f32[9,2,288]{2,1,0:T(2,128)S(1)}, f32[9,2,288]{2,1,0:T(2,128)}, u32[]{:S(2)}) copy-start(f32[9,2,288]{2,1,0:T(2,128)} %copy-done.5) | copy-start | bytes 62212
  575.6 11.3 %all-to-all-start.19 = ((f32[8,1,648]{2,1,0:T(1,128)}), f32[8,1,648]{2,1,0:T(1,128)S(1)}, u32[]{:S(2)}, u32[]{:S(2)}) async-start(f32[8,1,648]{2,1,0:T(1,128)} %reshape.432), calls=%async_computation.19 | async-start | bytes 49152 | tf_op jit(solution)/shard_map/all_to_all | solution.py:38
  588.2 8.5 %all-to-all-start.18 = ((f32[8,1,1]{2,1,0:T(1,128)}), f32[8,1,1]{2,1,0:T(1,128)S(1)}, u32[]{:S(2)}, u32[]{:S(2)}) async-start(f32[8,1,1]{2,1,0:T(1,128)} %broadcast_in_dim.113), calls=%async_computation.18 | async-start | bytes 8192 | tf_op jit(solution)/shard_map/all_to_all | solution.py:16
  596.7 12.9 %all-to-all-start.20 = ((f32[32,1,648]{2,1,0:T(1,128)}), f32[32,1,648]{2,1,0:T(1,128)S(1)}, u32[]{:S(2)}, u32[]{:S(2)}) async-start(f32[32,1,648]{2,1,0:T(1,128)} %reshape.434), calls=%async_computation.20 | async-start | bytes 196608 | tf_op jit(solution)/shard_map/all_to_all | solution.py:16
  612.1 9.7 %all-to-all-start.21 = ((f32[8,1,648]{2,1,0:T(1,128)}), f32[8,1,648]{2,1,0:T(1,128)S(1)}, u32[]{:S(2)}, u32[]{:S(2)}) async-start(f32[8,1,648]{2,1,0:T(1,128)} %reshape.436), calls=%async_computation.21 | async-start | bytes 49152 | tf_op jit(solution)/shard_map/all_to_all | solution.py:16
where the time goes:
time: 636 us; the launch traced here: 624 us
  local copies, waits for them, and re-layouts  206 us (32%)
  matrix products  99.8 us (16%)
  waiting for transfers between devices  86.9 us (14%)
  starting transfers between devices  82 us (13%)
  blocking collectives  71.1 us (11%)
  other arithmetic  69.4 us (11%)
  between operations  6.71 us (1%)
    dynamic_update_slice x32, local copies, waits for them, and re-layouts, spread_cycles(): pieces = lax.map(one_block, cycle_ids.reshape(blocks, block))  110 us
    all_to_all x14, waiting for transfers between devices, sent_to_all(): return lax.all_to_all(copies, axis, split_axis=0, concat_axis=0, tiled=True)  78.9 us
    all_to_all x14, starting transfers between devices, sent_to_all(): return lax.all_to_all(copies, axis, split_axis=0, concat_axis=0, tiled=True)  69 us
    dynamic_slice x64, local copies, waits for them, and re-layouts, collect_cycles(): lax.scan(add_block, jnp.zeros((rows, cycle_count), jnp.float32), (cycle_i...  47 us
    dot_general x16, matrix products, one_block(): jnp.dot(onehot, flat_cycles.T, precision=PRECISE, preferred_element_type=...  40.8 us
    dot_general x24, matrix products, add_block(): jnp.dot(value_block, onehot, precision=PRECISE, preferred_element_type=jn...  36.9 us
    all_to_all x3, blocking collectives, summed_on_arrival(): lax.all_to_all(in_blocks(array, dim, devices), axis, 0, 0, tiled=True)  36.9 us
    all_to_all x3, blocking collectives, sent_to_all(): return lax.all_to_all(copies, axis, split_axis=0, concat_axis=0, tiled=True)  34.3 us
  transfers between devices with their start and end apart: 16, of which 16 were waited for; matrix products, arithmetic and copies ran while one was open for 3% of the time, Pallas kernels for 0%

commit v1 on v0

v1 whole, which is shorter than its diff:
```python
import functools

import jax
import jax.numpy as jnp
from jax import lax
from jax.experimental import pallas as pl
from jax.experimental.pallas import tpu as pltpu
from jax.sharding import PartitionSpec as P

ITERS = 2
MESH = pl.DeviceIdType.MESH
LANES = 128
SLOTS = 256
CYCLES_HERE = 8
GROUP = 20
GROUPS = 5
SHARE = 8 * GROUPS
SCALAR_LANE = 127
CURVE_COLUMN = 18
TWO_OVER_PI = 0.6366197723675814
PI_2_A = 1.5703125
PI_2_B = 0.00048351287841796875
PI_2_C = 3.13855707645416259765625e-07
PI_2_D = 6.077100628276710e-11


def sine_cosine(angle):
    turns = jnp.floor(angle * TWO_OVER_PI + 0.5)
    rest = angle - turns * PI_2_A
    rest = rest - turns * PI_2_B
    rest = rest - turns * PI_2_C
    rest = rest - turns * PI_2_D
    square = rest * rest
    sine = rest + rest * square * (-1.6666654611e-1 + square * (8.3321608736e-3 + square * -1.9515295891e-4))
    cosine = 1.0 - 0.5 * square + square * square * (
        4.166664568298827e-2 + square * (-1.388731625493765e-3 + square * 2.443315711809948e-5)
    )
    quadrant = turns.astype(jnp.int32)
    swap = (quadrant & 1) == 1
    sine_out = jnp.where(swap, cosine, sine)
    cosine_out = jnp.where(swap, sine, cosine)
    sine_out = jnp.where((quadrant & 2) == 2, -sine_out, sine_out)
    cosine_out = jnp.where(((quadrant + 1) & 2) == 2, -cosine_out, cosine_out)
    return sine_out, cosine_out


def prologue_kernel(total_obs, count_ref, cycle_ref, lon_ref, obs_ref, weight_ref, lon_out, scale_out, first_out):
    first_cycle = lax.axis_index("ord") * CYCLES_HERE
    rows = cycle_ref.shape[0]
    ids = cycle_ref[...]
    starts = []
    for step in range(CYCLES_HERE + 1):
        below = jnp.where(ids < first_cycle + step, 1.0, 0.0)
        starts.append(jnp.sum(below).astype(jnp.int32))
    lane = lax.broadcasted_iota(jnp.int32, (1, LANES), 1)
    used = count_ref[0]
    for step in range(CYCLES_HERE):
        start = starts[step]
        count = starts[step + 1] - start
        row = start // LANES
        shift = start - row * LANES
        turn = lax.rem(LANES - shift, LANES)
        lines = [jnp.minimum(row + part, rows - 1) for part in range(3)]
        head = lane < LANES - shift
        windows = []
        for ref in (lon_ref, obs_ref, weight_ref):
            turned = [pltpu.roll(ref[pl.ds(line, 1), :], turn, 1) for line in lines]
            windows.append([jnp.where(head, turned[part], turned[part + 1]) for part in range(2)])
        for part in range(2):
            slot = lane + part * LANES
            valid = jnp.logical_and(slot < count, start + slot < used)
            scale = jnp.where(valid, windows[2][part] / total_obs, 0.0)
            cut = pl.ds(part * LANES, LANES)
            lon_out[pl.ds(step, 1), cut] = windows[0][part]
            scale_out[pl.ds(step, 1), cut] = scale
            first_out[pl.ds(step, 1), cut] = scale * windows[1][part]


def offset(index):
    return ((index + 1) // 2) * (1 - 2 * (index % 2))


def main_kernel(
    dims, own_ref, lon_ref, scale_ref, first_ref, leg_hbm, inv_hbm, solution_ref, residual_ref,
    harm, leg, inv, column, rows_ref, tile_send, tile_recv, part_send, part_recv, share_send, share_recv,
    all_send, all_recv, ids_send, ids_recv, ids_smem, slot_smem, local_sem, send_sem, recv_sem,
):
    block, degrees, cycles, ord_y, ord_z, obs_x = dims
    ords = ord_y * ord_z
    obss = obs_x * 2
    columns = 2 * block
    ord_here = lax.axis_index("ord")
    obs_here = lax.axis_index("obs")

    for slot in range(block):
        inv[slot, pl.ds(degrees, SHARE * obss - degrees), :] = jnp.zeros((SHARE * obss - degrees, degrees), jnp.float32)
    leg_copy = pltpu.make_async_copy(leg_hbm, leg, local_sem.at[0])
    inv_copy = pltpu.make_async_copy(inv_hbm, inv.at[:, pl.ds(0, degrees), :], local_sem.at[1])
    leg_copy.start()
    inv_copy.start()

    def ord_peer(index):
        step_y = ord_y // 2 + offset(index // ord_z)
        step_z = ord_z // 2 + offset(index % ord_z)
        here_y = ord_here // ord_z
        here_z = ord_here % ord_z
        return ((here_y + step_y) % ord_y) * ord_z + (here_z + step_z) % ord_z

    def obs_peer(index):
        step_x = obs_x // 2 + offset(index // 2)
        step_core = 1 - index % 2
        return ((obs_here // 2 + step_x) % obs_x) * 2 + (obs_here % 2 + step_core) % 2

    barrier = pltpu.get_barrier_semaphore()

    def greet_ord(index, carry):
        pl.semaphore_signal(barrier, inc=1, device_id={"ord": ord_peer(index)}, device_id_type=MESH)
        return carry

    def greet_obs(index, carry):
        pl.semaphore_signal(barrier, inc=1, device_id={"obs": obs_peer(index)}, device_id_type=MESH)
        return carry

    lax.fori_loop(0, ords - 1, greet_ord, 0)
    lax.fori_loop(0, obss - 1, greet_obs, 0)

    lane = lax.broadcasted_iota(jnp.int32, (8, LANES), 1)
    sublane = lax.broadcasted_iota(jnp.int32, (8, LANES), 0)
    group = lane // GROUP
    inner = lane % GROUP
    slot_lane = inner // 2
    degree_here = obs_here * SHARE + group * 8 + sublane
    inside = jnp.logical_and(jnp.logical_and(group < GROUPS, inner < columns), degree_here < degrees)
    order_lane = jnp.zeros((8, LANES), jnp.int32)
    for slot in range(block):
        order_lane = jnp.where(slot_lane == slot, own_ref[slot], order_lane)
    live = jnp.logical_and(inside, degree_here >= order_lane)

    ids_row = jnp.zeros((1, LANES), jnp.int32)
    lane_row = lax.broadcasted_iota(jnp.int32, (1, LANES), 1)
    for slot in range(block):
        ids_row = jnp.where(lane_row == slot, own_ref[slot], ids_row)
    ids_send[...] = ids_row
    ids_recv[ord_here] = ids_row
    for which in range(len(rows_ref)):
        rows_ref[which][...] = jnp.zeros((32, cycles), jnp.float32)
    column[...] = jnp.zeros(column.shape, jnp.float32)

    longitude = lon_ref[...]

    def harmonic_block(index, carry):
        for order in range(block):
            number = (index * block + order).astype(jnp.float32)
            sine, cosine = sine_cosine(number * longitude)
            harm[index, 2 * order] = cosine
            harm[index, 2 * order + 1] = sine
        return carry

    lax.fori_loop(0, ords, harmonic_block, 0)
    pl.semaphore_wait(barrier, ords - 1 + obss - 1)

    rounds = [0]
    waits = []

    def next_round():
        rounds[0] += 1
        return rounds[0] - 1

    def ord_copy(source, target, sems, peer):
        return pltpu.make_async_remote_copy(
            src_ref=source, dst_ref=target, send_sem=send_sem.at[sems], recv_sem=recv_sem.at[sems],
            device_id={"ord": peer}, device_id_type=MESH,
        )

    def obs_copy(source, target, sems, peer):
        return pltpu.make_async_remote_copy(
            src_ref=source, dst_ref=target, send_sem=send_sem.at[sems], recv_sem=recv_sem.at[sems],
            device_id={"obs": peer}, device_id_type=MESH,
        )

    def whole(make, buffer, sems, peers, peer):
        cut = buffer.at[pl.ds(0, peers)]
        return make(cut, cut, sems, peer)

    def gather_ord(source, buffer):
        sems = next_round()

        def send(index, carry):
            ord_copy(source, buffer.at[ord_here], sems, ord_peer(index)).start()
            return carry

        lax.fori_loop(0, ords - 1, send, 0)
        done = whole(ord_copy, buffer, sems, ords - 1, ord_peer(0))
        waits.append(done)
        return done

    def gather_obs(source, buffer):
        sems = next_round()

        def send(index, carry):
            obs_copy(source, buffer.at[obs_here], sems, obs_peer(index)).start()
            return carry

        lax.fori_loop(0, obss - 1, send, 0)
        done = whole(obs_copy, buffer, sems, obss - 1, obs_peer(0))
        waits.append(done)
        return done

    ids_done = gather_ord(ids_send, ids_recv)

    tiles = [0]
    parts = [0]
    shares = [0]
    alls = [0]

    def per_cycle(weighted, curve):
        which = tiles[0]
        tiles[0] += 1
        sems = next_round()
        send_buf, recv_buf = tile_send[which], tile_recv[which]
        corner = jnp.logical_and(lane == CURVE_COLUMN, sublane == 0)
        empty = jnp.where(corner, curve, 0.0)

        def step(outer, carry):
            for inner_step in range(4):
                index = outer * 4 + inner_step
                peer = ord_peer(index)
                tile = empty
                for col in range(columns):
                    total = jnp.sum(harm[peer, col] * weighted, axis=1, keepdims=True)
                    tile = jnp.where(lane == col, total, tile)
                send_buf[peer] = tile
                if inner_step < 3:
                    ord_copy(send_buf.at[peer], recv_buf.at[ord_here], sems, peer).start()
                else:
                    @pl.when(index < ords - 1)
                    def _():
                        ord_copy(send_buf.at[peer], recv_buf.at[ord_here], sems, peer).start()

                    @pl.when(index == ords - 1)
                    def _():
                        recv_buf[ord_here] = tile
            return carry

        lax.fori_loop(0, ords // 4, step, 0)
        done = whole(ord_copy, recv_buf, sems, ords - 1, ord_peer(0))
        waits.append(done)
        return done, recv_buf

    def adjoint(recv_buf, rows):
        per_order = jnp.transpose(recv_buf[...].reshape(cycles, LANES)[:, :32])
        rows[...] = per_order
        curve = jnp.sum(rows[pl.ds(CURVE_COLUMN, 1), :], axis=1, keepdims=True)
        lane_all = lax.broadcasted_iota(jnp.int32, (degrees, LANES), 1)
        total = jnp.zeros((degrees, LANES), jnp.float32)
        for order in range(block):
            table = leg[order]
            for part in range(2):
                col = 2 * order + part
                value = jnp.sum(table * rows[pl.ds(col, 1), :], axis=1, keepdims=True)
                total = jnp.where(lane_all == col, value, total)
        column[pl.ds(0, degrees), :] = total
        which = parts[0]
        parts[0] += 1
        send_buf, recv_obs = part_send[which], part_recv[which]
        for owner in range(obss):
            packed = jnp.where(lane == SCALAR_LANE, curve, 0.0)
            for piece in range(GROUPS):
                start = owner * SHARE + piece * 8
                if start < degrees:
                    lines = column[pl.ds(start, 8), :]
                    packed = packed + (pltpu.roll(lines, GROUP * piece, 1) if piece else lines)
            send_buf[owner] = packed
        sems = next_round()

        def send(index, carry):
            peer = obs_peer(index)
            obs_copy(send_buf.at[peer], recv_obs.at[obs_here], sems, peer).start()
            return carry

        lax.fori_loop(0, obss - 1, send, 0)
        recv_obs[obs_here] = send_buf[obs_here]
        done = whole(obs_copy, recv_obs, sems, obss - 1, obs_peer(0))
        waits.append(done)
        done.wait_recv()
        summed = jnp.sum(recv_obs[...], axis=0)
        return summed, summed[0:1, SCALAR_LANE : SCALAR_LANE + 1]

    def exchange_ord(packed, index_ref):
        which = shares[0]
        shares[0] += 1
        send_buf, recv_buf = share_send[which], share_recv[which]
        send_buf[...] = packed
        recv_buf[ord_here] = packed
        gather_ord(send_buf, recv_buf).wait_recv()
        everyone = jnp.sum(recv_buf[...], axis=0)
        chosen = jnp.where(lane == SCALAR_LANE, everyone, 0.0)
        for slot in range(block):
            number = index_ref[slot]
            source = number // block
            place = number - source * block
            turn = lax.rem(2 * slot - 2 * place + LANES, LANES)
            lines = pltpu.roll(recv_buf[source], turn, 1)
            chosen = jnp.where(jnp.logical_and(inside, slot_lane == slot), lines, chosen)
        return chosen

    def exchange_obs(packed):
        which = alls[0]
        alls[0] += 1
        send_buf, recv_buf = all_send[which], all_recv[which]
        send_buf[...] = packed
        recv_buf[obs_here] = packed
        gather_obs(send_buf, recv_buf).wait_recv()
        total = jnp.sum(recv_buf[...], axis=0)[0:1, SCALAR_LANE : SCALAR_LANE + 1]
        pieces = []
        for owner in range(obss):
            for piece in range(GROUPS):
                if owner * SHARE + piece * 8 < degrees:
                    lines = recv_buf[owner]
                    pieces.append(pltpu.roll(lines, LANES - GROUP * piece, 1) if piece else lines)
        return jnp.concatenate(pieces, axis=0), total

    def precondition(packed):
        lines, unused = exchange_obs(packed)
        column[pl.ds(0, degrees), :] = lines
        by_slot = jnp.transpose(column[...])
        start = pl.multiple_of(obs_here * SHARE, 8)
        result = jnp.zeros((8, LANES), jnp.float32)
        for slot in range(block):
            table = inv[slot, pl.ds(start, SHARE), :]
            for part in range(2):
                col = 2 * slot + part
                value = jnp.sum(table * by_slot[col : col + 1, :degrees], axis=1, keepdims=True)
                for piece in range(GROUPS):
                    result = jnp.where(lane == GROUP * piece + col, value[8 * piece : 8 * piece + 8], result)
        return jnp.where(live, result, 0.0)

    def with_energy(residual, precond):
        product = jnp.where(inside, residual * precond, 0.0)
        share = jnp.sum(jnp.sum(product, axis=1, keepdims=True), axis=0, keepdims=True)
        return jnp.where(lane == SCALAR_LANE, share, precond)

    def synthesize(coefficients, rows):
        which = tiles[0]
        tiles[0] += 1
        sems = next_round()
        send_buf, recv_buf = tile_send[which], tile_recv[which]
        for order in range(block):
            table = leg[order]
            for part in range(2):
                col = 2 * order + part
                rows[pl.ds(col, 1), :] = jnp.sum(table * coefficients[:, col : col + 1], axis=0, keepdims=True)
        turned = jnp.transpose(rows[...]).reshape(ords, CYCLES_HERE, 32)
        send_buf[:, :, pl.ds(0, 32)] = turned
        recv_buf[ord_here] = send_buf[ord_here]

        def send(index, carry):
            peer = ord_peer(index)
            ord_copy(send_buf.at[peer], recv_buf.at[ord_here], sems, peer).start()
            return carry

        lax.fori_loop(0, ords - 1, send, 0)
        done = whole(ord_copy, recv_buf, sems, ords - 1, ord_peer(0))
        waits.append(done)
        done.wait_recv()

        def step(outer, sums):
            sums = list(sums)
            for inner_step in range(4):
                index = outer * 4 + inner_step
                tile = recv_buf[index]
                for col in range(columns):
                    sums[col % 2] = sums[col % 2] + harm[index, col] * tile[:, col : col + 1]
            return tuple(sums)

        zero = jnp.zeros((CYCLES_HERE, SLOTS), jnp.float32)
        sums = lax.fori_loop(0, ords // 4, step, (zero, zero))
        return sums[0] + sums[1]

    leg_copy.wait()
    done, recv_buf = per_cycle(first_ref[...], jnp.zeros((1, 1), jnp.float32))

    ids_done.wait_recv()
    ids_copy = pltpu.make_async_copy(ids_recv, ids_smem, local_sem.at[2])
    ids_copy.start()
    ids_copy.wait()
    first_order = ord_here * block

    def find(owner, found):
        found = list(found)
        for slot in range(block):
            number = ids_smem[owner, 0, slot]
            for order in range(block):
                found[order] = jnp.where(number == first_order + order, owner * block + slot, found[order])
        return tuple(found)

    found = lax.fori_loop(0, ords, find, tuple(jnp.int32(0) for unused in range(block)))
    for order in range(block):
        slot_smem[order] = found[order]
    inv_copy.wait()

    done.wait_recv()
    summed, unused = adjoint(recv_buf, rows_ref[0])
    residual = exchange_ord(summed, own_ref)
    residual = jnp.where(inside, residual, 0.0)
    precond = precondition(residual)
    solution = jnp.zeros((8, LANES), jnp.float32)
    direction = None
    coefficients = None
    energy_now = None
    for iteration in range(ITERS):
        chosen = exchange_ord(with_energy(residual, precond), slot_smem)
        lines, energy = exchange_obs(chosen)
        if iteration == 0:
            direction, coefficients = precond, lines
        else:
            ratio = energy / energy_now
            direction = precond + ratio * direction
            coefficients = lines + ratio * coefficients
        energy_now = energy
        gradient = synthesize(coefficients, rows_ref[1])
        weighted = scale_ref[...] * gradient
        curve = jnp.sum(jnp.sum(weighted * gradient, axis=1, keepdims=True), axis=0, keepdims=True)
        done, recv_buf = per_cycle(weighted, curve)
        done.wait_recv()
        summed, curvature = adjoint(recv_buf, rows_ref[0])
        image = jnp.where(inside, exchange_ord(summed, own_ref), 0.0)
        step_size = energy_now / curvature
        solution = solution + step_size * direction
        residual = residual - step_size * image
        if iteration + 1 < ITERS:
            precond = precondition(residual)

    for value, out in ((solution, solution_ref), (residual, residual_ref)):
        lines, unused = exchange_obs(value)
        column[pl.ds(0, degrees), :] = lines
        by_slot = jnp.transpose(column[...])
        for slot in range(block):
            out[slot] = by_slot[2 * slot : 2 * slot + 2, :degrees]
    for done in waits:
        done.wait_send()


def buffers(rounds, *shape):
    return [pltpu.VMEM(shape, jnp.float32) for unused in range(rounds)]


def body(ord_y, ord_z, obs_x, longitude, cycle_of, obs_count, observed, obs_weight, legendre, precond_inv, order_of_slot):
    block, degrees, cycles = legendre.shape[1:]
    slab = longitude.shape[1]
    ords, obss = ord_y * ord_z, obs_x * 2
    vmem = pl.BlockSpec(memory_space=pltpu.VMEM)
    smem = pl.BlockSpec(memory_space=pltpu.SMEM)
    hbm = pl.BlockSpec(memory_space=pl.ANY)
    window = jax.ShapeDtypeStruct((CYCLES_HERE, SLOTS), jnp.float32)
    lines = (slab // LANES, LANES)
    east, scale, first = pl.pallas_call(
        functools.partial(prologue_kernel, float(slab * obss)),
        out_shape=(window, window, window),
        in_specs=[smem, vmem, vmem, vmem, vmem],
        out_specs=(vmem, vmem, vmem),
        name="windows",
    )(obs_count, cycle_of.reshape(lines), longitude.reshape(lines), observed.reshape(lines), obs_weight.reshape(lines))
    result = jax.ShapeDtypeStruct((block, 2, degrees), jnp.float32)
    dims = (block, degrees, cycles, ord_y, ord_z, obs_x)
    column_rows = -(-max(degrees, 1) // LANES) * LANES
    tile_rounds = 1 + 2 * ITERS
    share_rounds = 1 + 2 * ITERS
    all_rounds = 2 * ITERS + 2
    total_rounds = 1 + tile_rounds + (1 + ITERS) + share_rounds + all_rounds
    scratch = [
        pltpu.VMEM((ords, 2 * block, CYCLES_HERE, SLOTS), jnp.float32),
        pltpu.VMEM((block, degrees, cycles), jnp.float32),
        pltpu.VMEM((block, SHARE * obss, degrees), jnp.float32),
        pltpu.VMEM((column_rows, LANES), jnp.float32),
        [pltpu.VMEM((32, cycles), jnp.float32), pltpu.VMEM((32, cycles), jnp.float32)],
        buffers(tile_rounds, ords, CYCLES_HERE, LANES),
        buffers(tile_rounds, ords, CYCLES_HERE, LANES),
        buffers(1 + ITERS, obss, 8, LANES),
        buffers(1 + ITERS, obss, 8, LANES),
        buffers(share_rounds, 8, LANES),
        buffers(share_rounds, ords, 8, LANES),
        buffers(all_rounds, 8, LANES),
        buffers(all_rounds, obss, 8, LANES),
        pltpu.VMEM((1, LANES), jnp.int32),
        pltpu.VMEM((ords, 1, LANES), jnp.int32),
        pltpu.SMEM((ords, 1, LANES), jnp.int32),
        pltpu.SMEM((block,), jnp.int32),
        pltpu.SemaphoreType.DMA((3,)),
        pltpu.SemaphoreType.DMA((total_rounds,)),
        pltpu.SemaphoreType.DMA((total_rounds,)),
    ]
    return pl.pallas_call(
        functools.partial(main_kernel, dims),
        out_shape=(result, result),
        in_specs=[smem, vmem, vmem, vmem, hbm, hbm],
        out_specs=(vmem, vmem),
        scratch_shapes=scratch,
        compiler_params=pltpu.CompilerParams(
            collective_id=0, has_side_effects=True, vmem_limit_bytes=48 * 1024 * 1024
        ),
        name="solve",
    )(order_of_slot, east, scale, first, legendre[0], precond_inv)


def solution(mesh):
    placed = (
        P("obs", None),
        P("obs", None),
        P("obs"),
        P("obs", None),
        P("obs", None),
        P("obs", "ord", None, None),
        P("ord", None, None),
        P("ord"),
    )
    ords = mesh.shape["ord"]
    ord_y = 4 if ords == 32 else 2
    run = functools.partial(body, ord_y, ords // ord_y, mesh.shape["obs"] // 2)
    return jax.shard_map(
        run,
        mesh=mesh,
        in_specs=placed,
        out_specs=(P("ord", None, None), P("ord", None, None)),
        check_vma=False,
    )
```

time: 636 us -> 135 us (0.21); the launches traced: 624 us -> 135 us
  local copies, waits for them, and re-layouts: 206 us -> 5.71 us
  Pallas kernels: 0 us -> 128 us
  matrix products: 99.8 us -> 0 us
  waiting for transfers between devices: 86.9 us -> 0 us
  starting transfers between devices: 82 us -> 0 us
  blocking collectives: 71.1 us -> 0 us
  other arithmetic: 69.4 us -> 0 us
    pallas_call x0 -> x2, Pallas kernels: none -> 128 us  [the longest x1 126 us: body(): pl.pallas_call(functools.partial(main_kernel, dims), out_shape=(result, r...]
    dynamic_update_slice x32 -> x0, local copies, waits for them, and re-layouts: 110 us -> none  [spread_cycles(): pieces = lax.map(one_block, cycle_ids.reshape(blocks, block))]
    dot_general x47 -> x0, matrix products: 99.8 us -> none  [the longest x16 40.8 us: one_block(): jnp.dot(onehot, flat_cycles.T, precision=PRECISE, preferred_element_type=...]
    all_to_all x16 -> x0, waiting for transfers between devices: 86.9 us -> none  [the longest x14 78.9 us: sent_to_all(): return lax.all_to_all(copies, axis, split_axis=0, concat_axis=0, tiled=True)]
    all_to_all x16 -> x0, starting transfers between devices: 82 us -> none  [the longest x14 69 us: sent_to_all(): return lax.all_to_all(copies, axis, split_axis=0, concat_axis=0, tiled=True)]
    all_to_all x6 -> x0, blocking collectives: 71.1 us -> none  [the longest x3 36.9 us: summed_on_arrival(): lax.all_to_all(in_blocks(array, dim, devices), axis, 0, 0, tiled=True)]
    dynamic_slice x66 -> x0, local copies, waits for them, and re-layouts: 47.2 us -> none  [the longest x64 47 us: collect_cycles(): lax.scan(add_block, jnp.zeros((rows, cycle_count), jnp.float32), (cycle_i...]
    cos x1 -> x0, other arithmetic: 34.1 us -> none  [body(): harmonic = jnp.stack([jnp.cos(angles), jnp.sin(angles)], axis=1)]
  transfers between devices with their start and end apart: 16 -> 0, of which waited for: 16 -> 0; matrix products, arithmetic and copies ran while one was open for 3% -> 0% of each run, Pallas kernels for 0% -> 0%
where the time goes in v1:
time: 135 us
  Pallas kernels  128 us (95%)
  local copies, waits for them, and re-layouts  5.71 us (4%)
    pallas_call x1, Pallas kernels, body(): pl.pallas_call(functools.partial(main_kernel, dims), out_shape=(result, r...  126 us
    unnamed x12, local copies, waits for them, and re-layouts  5.71 us

profile of v1, /device:TPU:1, one launch (start us, length us, event | category | flops | bytes accessed | tf_op | source)
XLA Modules:
  0.0 135.1 jit_solution(455626119960784145)
XLA Ops:
  1.3 2.1 %windows.1 = (f32[8,256]{1,0:T(8,128)}, f32[8,256]{1,0:T(8,128)}, f32[8,256]{1,0:T(8,128)}) custom-call(s32[1]{0:T(128)S(6)} %copy.12.count_ref, s32[256,128]{1,0:T(8,128)} %bitcast.6, f32[256,128]{1,0:T(8,128)} %bitcast.7, f32[256,128]{1,0:T(8,128)} %bitcast.8, f32[256,128]{1,0:T(8,128)} %bitcast.9), custom_call_target="tpu_custom_call" | custom-call | tf_op jit(solution)/shard_map/windows/pallas_call | solution.py:457
  3.3 0.0 copy-start
  3.3 1.7 %copy-done = f32[1,9,288,256]{3,2,1,0:T(8,128)S(1)} copy-done((f32[1,9,288,256]{3,2,1,0:T(8,128)S(1)}, f32[1,9,288,256]{3,2,1,0:T(8,128)}, u32[]{:S(2)}) %copy-start) | copy-done | bytes 2654232
  5.1 0.0 copy-start.1
  5.1 0.7 copy-done.1
  5.8 0.0 copy-start.2
  5.8 0.7 copy-done.2
  6.5 0.0 copy-start.3
  6.5 0.7 copy-done.3
  7.2 0.0 copy-start.4
  7.2 0.7 copy-done.4
  7.8 126.0 %solve.1 = (f32[9,2,288]{2,1,0:T(2,128)S(1)}, f32[9,2,288]{2,1,0:T(2,128)S(1)}) custom-call(s32[9]{0:T(128)S(1)} %copy-done.4, f32[8,256]{1,0:T(8,128)S(1)} %copy-done.1, f32[8,256]{1,0:T(8,128)S(1)} %copy-done.2, f32[8,256]{1,0:T(8,128)S(1)} %copy-done.3, f32[9,288,256]{2,1,0:T(8,128)S(1)} %bitcast.5, f32[9,288,288]{2,1,0:T(8,128)} %inv_hbm.1), custom_call_target="tpu_custom_call" | custom-call | tf_op jit(solution)/shard_map/solve/pallas_call | solution.py:493
  133.9 0.6 copy.13
  134.5 0.6 copy.14
Async XLA Ops:
  3.3 1.8 %copy-start = (f32[1,9,288,256]{3,2,1,0:T(8,128)S(1)}, f32[1,9,288,256]{3,2,1,0:T(8,128)}, u32[]{:S(2)}) copy-start(f32[1,9,288,256]{3,2,1,0:T(8,128)} %param.13) | copy-start | bytes 7962628
  5.1 0.7 copy-start.1
  5.8 0.7 copy-start.2
  6.5 0.7 copy-start.3
  7.2 0.7 copy-start.4

commit v2 on v1

--- a/solution.py
+++ b/solution.py
@@ -44,7 +44,7 @@
     return sine_out, cosine_out
 
 
-def prologue_kernel(total_obs, count_ref, cycle_ref, lon_ref, obs_ref, weight_ref, lon_out, scale_out, first_out):
+def prologue_kernel(total_obs, count_ref, cycle_ref, lon_ref, obs_ref, weight_ref, out_ref):
     first_cycle = lax.axis_index("ord") * CYCLES_HERE
     rows = cycle_ref.shape[0]
     ids = cycle_ref[...]
@@ -71,9 +71,8 @@
             valid = jnp.logical_and(slot < count, start + slot < used)
             scale = jnp.where(valid, windows[2][part] / total_obs, 0.0)
             cut = pl.ds(part * LANES, LANES)
-            lon_out[pl.ds(step, 1), cut] = windows[0][part]
-            scale_out[pl.ds(step, 1), cut] = scale
-            first_out[pl.ds(step, 1), cut] = scale * windows[1][part]
+            for which, value in enumerate((windows[0][part], scale, scale * windows[1][part])):
+                out_ref[pl.ds(which * CYCLES_HERE + step, 1), cut] = value
 
 
 def offset(index):
@@ -81,7 +80,7 @@
 
 
 def main_kernel(
-    dims, own_ref, lon_ref, scale_ref, first_ref, leg_hbm, inv_hbm, solution_ref, residual_ref,
+    dims, own_ref, windows_ref, leg_hbm, inv_hbm, solution_ref, residual_ref,
     harm, leg, inv, column, rows_ref, tile_send, tile_recv, part_send, part_recv, share_send, share_recv,
     all_send, all_recv, ids_send, ids_recv, ids_smem, slot_smem, local_sem, send_sem, recv_sem,
 ):
@@ -89,6 +88,7 @@
     ords = ord_y * ord_z
     obss = obs_x * 2
     columns = 2 * block
+    unroll = 2 * ord_y
     ord_here = lax.axis_index("ord")
     obs_here = lax.axis_index("obs")
 
@@ -99,30 +99,26 @@
     leg_copy.start()
     inv_copy.start()
 
+    here_y, here_z = lax.div(ord_here, ord_z), lax.rem(ord_here, ord_z)
+    here_x, here_core = lax.div(obs_here, 2), lax.rem(obs_here, 2)
+
+    def ord_at(step_y, step_z):
+        return lax.rem(here_y + step_y, ord_y) * ord_z + lax.rem(here_z + step_z, ord_z)
+
     def ord_peer(index):
-        step_y = ord_y // 2 + offset(index // ord_z)
-        step_z = ord_z // 2 + offset(index % ord_z)
-        here_y = ord_here // ord_z
-        here_z = ord_here % ord_z
-        return ((here_y + step_y) % ord_y) * ord_z + (here_z + step_z) % ord_z
+        return ord_at(ord_y // 2 + offset(index % ord_y), ord_z // 2 + offset(index // ord_y))
 
     def obs_peer(index):
         step_x = obs_x // 2 + offset(index // 2)
         step_core = 1 - index % 2
-        return ((obs_here // 2 + step_x) % obs_x) * 2 + (obs_here % 2 + step_core) % 2
+        return lax.rem(here_x + step_x, obs_x) * 2 + lax.rem(here_core + step_core, 2)
 
     barrier = pltpu.get_barrier_semaphore()
 
-    def greet_ord(index, carry):
+    for index in range(ords - 1):
         pl.semaphore_signal(barrier, inc=1, device_id={"ord": ord_peer(index)}, device_id_type=MESH)
-        return carry
-
-    def greet_obs(index, carry):
+    for index in range(obss - 1):
         pl.semaphore_signal(barrier, inc=1, device_id={"obs": obs_peer(index)}, device_id_type=MESH)
-        return carry
-
-    lax.fori_loop(0, ords - 1, greet_ord, 0)
-    lax.fori_loop(0, obss - 1, greet_obs, 0)
 
     lane = lax.broadcasted_iota(jnp.int32, (8, LANES), 1)
     sublane = lax.broadcasted_iota(jnp.int32, (8, LANES), 0)
@@ -146,7 +142,7 @@
         rows_ref[which][...] = jnp.zeros((32, cycles), jnp.float32)
     column[...] = jnp.zeros(column.shape, jnp.float32)
 
-    longitude = lon_ref[...]
+    longitude = windows_ref[pl.ds(0, CYCLES_HERE), :]
 
     def harmonic_block(index, carry):
         for order in range(block):
@@ -206,8 +202,6 @@
         waits.append(done)
         return done
 
-    ids_done = gather_ord(ids_send, ids_recv)
-
     tiles = [0]
     parts = [0]
     shares = [0]
@@ -222,15 +216,17 @@
         empty = jnp.where(corner, curve, 0.0)
 
         def step(outer, carry):
-            for inner_step in range(4):
-                index = outer * 4 + inner_step
-                peer = ord_peer(index)
+            for inner_step in range(unroll):
+                index = outer * unroll + inner_step
+                peer = ord_at(
+                    ord_y // 2 + offset(inner_step % ord_y), ord_z // 2 + offset(outer * (unroll // ord_y) + inner_step // ord_y)
+                )
                 tile = empty
                 for col in range(columns):
                     total = jnp.sum(harm[peer, col] * weighted, axis=1, keepdims=True)
                     tile = jnp.where(lane == col, total, tile)
                 send_buf[peer] = tile
-                if inner_step < 3:
+                if inner_step < unroll - 1:
                     ord_copy(send_buf.at[peer], recv_buf.at[ord_here], sems, peer).start()
                 else:
                     @pl.when(index < ords - 1)
@@ -242,7 +238,7 @@
                         recv_buf[ord_here] = tile
             return carry
 
-        lax.fori_loop(0, ords // 4, step, 0)
+        lax.fori_loop(0, ords // unroll, step, 0)
         done = whole(ord_copy, recv_buf, sems, ords - 1, ord_peer(0))
         waits.append(done)
         return done, recv_buf
@@ -304,13 +300,17 @@
             chosen = jnp.where(jnp.logical_and(inside, slot_lane == slot), lines, chosen)
         return chosen
 
-    def exchange_obs(packed):
+    def send_obs(packed):
         which = alls[0]
         alls[0] += 1
         send_buf, recv_buf = all_send[which], all_recv[which]
         send_buf[...] = packed
         recv_buf[obs_here] = packed
-        gather_obs(send_buf, recv_buf).wait_recv()
+        return gather_obs(send_buf, recv_buf), recv_buf
+
+    def take_obs(sent):
+        done, recv_buf = sent
+        done.wait_recv()
         total = jnp.sum(recv_buf[...], axis=0)[0:1, SCALAR_LANE : SCALAR_LANE + 1]
         pieces = []
         for owner in range(obss):
@@ -319,6 +319,9 @@
                     lines = recv_buf[owner]
                     pieces.append(pltpu.roll(lines, LANES - GROUP * piece, 1) if piece else lines)
         return jnp.concatenate(pieces, axis=0), total
+
+    def exchange_obs(packed):
+        return take_obs(send_obs(packed))
 
     def precondition(packed):
         lines, unused = exchange_obs(packed)
@@ -354,32 +357,37 @@
         send_buf[:, :, pl.ds(0, 32)] = turned
         recv_buf[ord_here] = send_buf[ord_here]
 
-        def send(index, carry):
-            peer = ord_peer(index)
-            ord_copy(send_buf.at[peer], recv_buf.at[ord_here], sems, peer).start()
-            return carry
-
-        lax.fori_loop(0, ords - 1, send, 0)
-        done = whole(ord_copy, recv_buf, sems, ords - 1, ord_peer(0))
-        waits.append(done)
-        done.wait_recv()
-
-        def step(outer, sums):
-            sums = list(sums)
-            for inner_step in range(4):
-                index = outer * 4 + inner_step
-                tile = recv_buf[index]
-                for col in range(columns):
-                    sums[col % 2] = sums[col % 2] + harm[index, col] * tile[:, col : col + 1]
-            return tuple(sums)
-
-        zero = jnp.zeros((CYCLES_HERE, SLOTS), jnp.float32)
-        sums = lax.fori_loop(0, ords // 4, step, (zero, zero))
-        return sums[0] + sums[1]
+        half = ord_z // 2
+        sems = [sems] + [next_round() for unused in range(half)]
+
+        def send_line(peer, sem):
+            ord_copy(send_buf.at[peer], recv_buf.at[ord_here], sem, peer).start()
+
+        for far in range(half, -1, -1):
+            for step_z in ([far] if far in (0, half) else [far, ord_z - far]):
+                for step_y in range(ord_y - 1, -1, -1):
+                    if step_z or step_y:
+                        send_line(ord_at(step_y, step_z), sems[far])
+
+        sums = [jnp.zeros((CYCLES_HERE, SLOTS), jnp.float32) for unused in range(4)]
+        for far in range(half + 1):
+            steps = [far] if far in (0, half) else [far, ord_z - far]
+            peers = len(steps) * ord_y - (far == 0)
+            done = whole(ord_copy, recv_buf, sems[far], peers, ord_at(0, half))
+            waits.append(done)
+            done.wait_recv()
+            for step_z in steps:
+                for step_y in range(ord_y):
+                    index = ord_at(step_y, step_z)
+                    tile = recv_buf[index]
+                    for col in range(columns):
+                        sums[col % 4] = sums[col % 4] + harm[index, col] * tile[:, col : col + 1]
+        return (sums[0] + sums[1]) + (sums[2] + sums[3])
 
     leg_copy.wait()
-    done, recv_buf = per_cycle(first_ref[...], jnp.zeros((1, 1), jnp.float32))
-
+    done, recv_buf = per_cycle(windows_ref[pl.ds(2 * CYCLES_HERE, CYCLES_HERE), :], jnp.zeros((1, 1), jnp.float32))
+
+    ids_done = gather_ord(ids_send, ids_recv)
     ids_done.wait_recv()
     ids_copy = pltpu.make_async_copy(ids_recv, ids_smem, local_sem.at[2])
     ids_copy.start()
@@ -419,20 +427,23 @@
             coefficients = lines + ratio * coefficients
         energy_now = energy
         gradient = synthesize(coefficients, rows_ref[1])
-        weighted = scale_ref[...] * gradient
+        weighted = windows_ref[pl.ds(CYCLES_HERE, CYCLES_HERE), :] * gradient
         curve = jnp.sum(jnp.sum(weighted * gradient, axis=1, keepdims=True), axis=0, keepdims=True)
         done, recv_buf = per_cycle(weighted, curve)
         done.wait_recv()
         summed, curvature = adjoint(recv_buf, rows_ref[0])
-        image = jnp.where(inside, exchange_ord(summed, own_ref), 0.0)
         step_size = energy_now / curvature
         solution = solution + step_size * direction
+        if iteration + 1 == ITERS:
+            sent_solution = send_obs(solution)
+        image = jnp.where(inside, exchange_ord(summed, own_ref), 0.0)
         residual = residual - step_size * image
         if iteration + 1 < ITERS:
             precond = precondition(residual)
 
-    for value, out in ((solution, solution_ref), (residual, residual_ref)):
-        lines, unused = exchange_obs(value)
+    sent = [(sent_solution, solution_ref), (send_obs(residual), residual_ref)]
+    for exchange, out in sent:
+        lines, unused = take_obs(exchange)
         column[pl.ds(0, degrees), :] = lines
         by_slot = jnp.transpose(column[...])
         for slot in range(block):
@@ -451,14 +462,14 @@
     ords, obss = ord_y * ord_z, obs_x * 2
     vmem = pl.BlockSpec(memory_space=pltpu.VMEM)
     smem = pl.BlockSpec(memory_space=pltpu.SMEM)
-    hbm = pl.BlockSpec(memory_space=pl.ANY)
-    window = jax.ShapeDtypeStruct((CYCLES_HERE, SLOTS), jnp.float32)
+    hbm = pl.BlockSpec(memory_space=pltpu.HBM)
+    window = jax.ShapeDtypeStruct((3 * CYCLES_HERE, SLOTS), jnp.float32)
     lines = (slab // LANES, LANES)
-    east, scale, first = pl.pallas_call(
+    windows = pl.pallas_call(
         functools.partial(prologue_kernel, float(slab * obss)),
-        out_shape=(window, window, window),
+        out_shape=window,
         in_specs=[smem, vmem, vmem, vmem, vmem],
-        out_specs=(vmem, vmem, vmem),
+        out_specs=vmem,
         name="windows",
     )(obs_count, cycle_of.reshape(lines), longitude.reshape(lines), observed.reshape(lines), obs_weight.reshape(lines))
     result = jax.ShapeDtypeStruct((block, 2, degrees), jnp.float32)
@@ -467,7 +478,7 @@
     tile_rounds = 1 + 2 * ITERS
     share_rounds = 1 + 2 * ITERS
     all_rounds = 2 * ITERS + 2
-    total_rounds = 1 + tile_rounds + (1 + ITERS) + share_rounds + all_rounds
+    total_rounds = 1 + tile_rounds + (1 + ITERS) + share_rounds + all_rounds + ITERS * (ord_z // 2)
     scratch = [
         pltpu.VMEM((ords, 2 * block, CYCLES_HERE, SLOTS), jnp.float32),
         pltpu.VMEM((block, degrees, cycles), jnp.float32),
@@ -493,14 +504,14 @@
     return pl.pallas_call(
         functools.partial(main_kernel, dims),
         out_shape=(result, result),
-        in_specs=[smem, vmem, vmem, vmem, hbm, hbm],
+        in_specs=[smem, vmem, hbm, hbm],
         out_specs=(vmem, vmem),
         scratch_shapes=scratch,
         compiler_params=pltpu.CompilerParams(
-            collective_id=0, has_side_effects=True, vmem_limit_bytes=48 * 1024 * 1024
+            collective_id=0, has_side_effects=True
         ),
         name="solve",
-    )(order_of_slot, east, scale, first, legendre[0], precond_inv)
+    )(order_of_slot, windows, legendre[0], precond_inv)
 
 
 def solution(mesh):

time: 135 us -> 128 us (0.948)
  Pallas kernels: 128 us -> 124 us
  local copies, waits for them, and re-layouts: 5.71 us -> 2.72 us
    pallas_call x1, Pallas kernels: 126 us -> 122 us  [body(): pl.pallas_call(functools.partial(main_kernel, dims), out_shape=(result, r...]
    unnamed x12 -> x2, local copies, waits for them, and re-layouts: 5.71 us -> 2.72 us
where the time goes in v2:
time: 128 us
  Pallas kernels  124 us (97%)
  local copies, waits for them, and re-layouts  2.72 us (2%)
  between operations  1.29 us (1%)
    pallas_call x1, Pallas kernels, body(): pl.pallas_call(functools.partial(main_kernel, dims), out_shape=(result, r...  122 us
    unnamed x2, local copies, waits for them, and re-layouts  2.72 us

profile of v2, /device:TPU:1, one launch (start us, length us, event | category | flops | bytes accessed | tf_op | source)
XLA Modules:
  0.0 127.7 jit_solution(1575791084162565538)
XLA Ops:
  1.3 2.1 %windows.1.windows_ref = f32[24,256]{1,0:T(8,128)} custom-call(s32[1]{0:T(128)S(6)} %copy.12.count_ref, s32[256,128]{1,0:T(8,128)} %bitcast.6, f32[256,128]{1,0:T(8,128)} %bitcast.7, f32[256,128]{1,0:T(8,128)} %bitcast.8, f32[256,128]{1,0:T(8,128)} %bitcast.9), custom_call_target="tpu_custom_call" | custom-call | tf_op jit(solution)/shard_map/windows/pallas_call | solution.py:468
  3.3 121.6 %solve.1 = (f32[9,2,288]{2,1,0:T(2,128)}, f32[9,2,288]{2,1,0:T(2,128)}) custom-call(s32[9]{0:T(128)} %own_ref.1, f32[24,256]{1,0:T(8,128)} %windows.1.windows_ref, f32[9,288,256]{2,1,0:T(8,128)} %bitcast.5, f32[9,288,288]{2,1,0:T(8,128)} %inv_hbm.1), custom_call_target="tpu_custom_call" | custom-call | tf_op jit(solution)/shard_map/solve/pallas_call | solution.py:504
  124.9 1.4 %copy.13 = f32[9,2,288]{2,1,0:T(2,128)} copy(f32[9,2,288]{2,1,0:T(2,128)} %get-tuple-element.4) | data formatting | bytes 41472
  126.3 1.4 %copy.14 = f32[9,2,288]{2,1,0:T(2,128)} copy(f32[9,2,288]{2,1,0:T(2,128)} %get-tuple-element.5) | data formatting | bytes 41472

commit v3 on v2

--- a/solution.py
+++ b/solution.py
@@ -82,7 +82,8 @@
 def main_kernel(
     dims, own_ref, windows_ref, leg_hbm, inv_hbm, solution_ref, residual_ref,
     harm, leg, inv, column, rows_ref, tile_send, tile_recv, part_send, part_recv, share_send, share_recv,
-    all_send, all_recv, ids_send, ids_recv, ids_smem, slot_smem, local_sem, send_sem, recv_sem,
+    all_send, all_recv, ids_send, ids_recv, ids_smem, slot_vmem, slot_all, slot_smem, spread_send, spread_recv,
+    inv_send, inv_recv, inv_block, local_sem, send_sem, recv_sem,
 ):
     block, degrees, cycles, ord_y, ord_z, obs_x = dims
     ords = ord_y * ord_z
@@ -131,6 +132,7 @@
     for slot in range(block):
         order_lane = jnp.where(slot_lane == slot, own_ref[slot], order_lane)
     live = jnp.logical_and(inside, degree_here >= order_lane)
+    live_block = jnp.logical_and(inside, degree_here >= ord_here * block + slot_lane)
 
     ids_row = jnp.zeros((1, LANES), jnp.int32)
     lane_row = lax.broadcasted_iota(jnp.int32, (1, LANES), 1)
@@ -282,18 +284,22 @@
         summed = jnp.sum(recv_obs[...], axis=0)
         return summed, summed[0:1, SCALAR_LANE : SCALAR_LANE + 1]
 
-    def exchange_ord(packed, index_ref):
+    def send_ord(packed):
         which = shares[0]
         shares[0] += 1
         send_buf, recv_buf = share_send[which], share_recv[which]
         send_buf[...] = packed
         recv_buf[ord_here] = packed
-        gather_ord(send_buf, recv_buf).wait_recv()
+        return gather_ord(send_buf, recv_buf), recv_buf
+
+    def take_ord(sent, index_ref):
+        done, recv_buf = sent
+        done.wait_recv()
         everyone = jnp.sum(recv_buf[...], axis=0)
         chosen = jnp.where(lane == SCALAR_LANE, everyone, 0.0)
         for slot in range(block):
             number = index_ref[slot]
-            source = number // block
+            source = lax.div(number, block)
             place = number - source * block
             turn = lax.rem(2 * slot - 2 * place + LANES, LANES)
             lines = pltpu.roll(recv_buf[source], turn, 1)
@@ -323,27 +329,111 @@
     def exchange_obs(packed):
         return take_obs(send_obs(packed))
 
-    def precondition(packed):
+    def precondition(packed, table_of, alive):
         lines, unused = exchange_obs(packed)
         column[pl.ds(0, degrees), :] = lines
         by_slot = jnp.transpose(column[...])
-        start = pl.multiple_of(obs_here * SHARE, 8)
         result = jnp.zeros((8, LANES), jnp.float32)
         for slot in range(block):
-            table = inv[slot, pl.ds(start, SHARE), :]
+            table = table_of(slot)
             for part in range(2):
                 col = 2 * slot + part
-                value = jnp.sum(table * by_slot[col : col + 1, :degrees], axis=1, keepdims=True)
+                value = jnp.sum(table * by_slot[col : col + 1, : table.shape[1]], axis=1, keepdims=True)
                 for piece in range(GROUPS):
                     result = jnp.where(lane == GROUP * piece + col, value[8 * piece : 8 * piece + 8], result)
-        return jnp.where(live, result, 0.0)
+        return jnp.where(alive, result, 0.0)
+
+    share_start = pl.multiple_of(obs_here * SHARE, 8)
+
+    def owner_table(slot):
+        return inv[slot, pl.ds(share_start, SHARE), :]
+
+    tiles_wide = inv_block.shape[2] // LANES
+    spread_sems, inv_sems = next_round(), next_round()
+
+    def build_spread():
+        for slot in range(block):
+            for wide in range(tiles_wide):
+                width = min(LANES, degrees - wide * LANES)
+                for piece in range(GROUPS):
+                    lines = inv[slot, pl.ds(share_start + 8 * piece, 8), pl.ds(wide * LANES, width)]
+                    if width < LANES:
+                        lines = jnp.concatenate([lines, jnp.zeros((8, LANES - width), jnp.float32)], axis=1)
+                    for half in range(2):
+                        place = (wide * GROUPS + piece) * 2 + half
+                        spread_send[place % ords, slot, place // ords] = lines[4 * half : 4 * half + 4]
+        spread_recv[pl.ds(ord_here * block, block)] = spread_send[ord_here]
+
+    def send_spread(first, last):
+        def send(index, carry):
+            peer = ord_peer(index)
+            ord_copy(spread_send.at[peer], spread_recv.at[pl.ds(ord_here * block, block)], spread_sems, peer).start()
+            return carry
+
+        lax.fori_loop(first, last, send, 0)
+
+    def build_inv():
+        cut = spread_recv.at[pl.ds(0, (ords - 1) * block)]
+        done = ord_copy(cut, cut, spread_sems, ord_peer(0))
+        waits.append(done)
+        done.wait_recv()
+
+        def step(index, carry):
+            for order in range(block):
+                number = index * block + order
+                inv_send[index, order] = spread_recv[slot_all[lax.div(number, LANES), lax.rem(number, LANES)]]
+            return carry
+
+        lax.fori_loop(0, ords, step, 0)
+        inv_recv[ord_here] = inv_send[ord_here]
+
+    def send_inv(first, last):
+        def send(index, carry):
+            peer = ord_peer(index)
+            ord_copy(inv_send.at[peer], inv_recv.at[ord_here], inv_sems, peer).start()
+            return carry
+
+        lax.fori_loop(first, last, send, 0)
+
+    def take_inv():
+        done = whole(ord_copy, inv_recv, inv_sems, ords - 1, ord_peer(0))
+        waits.append(done)
+        done.wait_recv()
+        for order in range(block):
+            for wide in range(tiles_wide):
+                for piece in range(GROUPS):
+                    for half in range(2):
+                        place = (wide * GROUPS + piece) * 2 + half
+                        inv_block[order, pl.ds(8 * piece + 4 * half, 4), pl.ds(wide * LANES, LANES)] = inv_recv[
+                            place % ords, order, place // ords
+                        ]
+
+    def find_slots():
+        ids_done.wait_recv()
+        ids_copy = pltpu.make_async_copy(ids_recv, ids_smem, local_sem.at[2])
+        ids_copy.start()
+        ids_copy.wait()
+        position = sublane * LANES + lane
+
+        def find(owner, found):
+            for slot in range(block):
+                found = jnp.where(position == ids_smem[owner, 0, slot], owner * block + slot, found)
+            return found
+
+        slot_vmem[...] = lax.fori_loop(0, ords, find, jnp.zeros((8, LANES), jnp.int32))
+        slot_copy = pltpu.make_async_copy(slot_vmem, slot_all, local_sem.at[3])
+        slot_copy.start()
+        slot_copy.wait()
+        for order in range(block):
+            number = ord_here * block + order
+            slot_smem[order] = slot_all[lax.div(number, LANES), lax.rem(number, LANES)]
 
     def with_energy(residual, precond):
         product = jnp.where(inside, residual * precond, 0.0)
         share = jnp.sum(jnp.sum(product, axis=1, keepdims=True), axis=0, keepdims=True)
         return jnp.where(lane == SCALAR_LANE, share, precond)
 
-    def synthesize(coefficients, rows):
+    def synthesize(coefficients, energy, rows, meanwhile):
         which = tiles[0]
         tiles[0] += 1
         sems = next_round()
@@ -353,6 +443,7 @@
             for part in range(2):
                 col = 2 * order + part
                 rows[pl.ds(col, 1), :] = jnp.sum(table * coefficients[:, col : col + 1], axis=0, keepdims=True)
+        rows[pl.ds(CURVE_COLUMN, 1), :] = jnp.broadcast_to(energy, (1, cycles))
         turned = jnp.transpose(rows[...]).reshape(ords, CYCLES_HERE, 32)
         send_buf[:, :, pl.ds(0, 32)] = turned
         recv_buf[ord_here] = send_buf[ord_here]
@@ -369,7 +460,9 @@
                     if step_z or step_y:
                         send_line(ord_at(step_y, step_z), sems[far])
 
+        meanwhile()
         sums = [jnp.zeros((CYCLES_HERE, SLOTS), jnp.float32) for unused in range(4)]
+        energies = jnp.zeros((8, LANES), jnp.float32)
         for far in range(half + 1):
             steps = [far] if far in (0, half) else [far, ord_z - far]
             peers = len(steps) * ord_y - (far == 0)
@@ -380,68 +473,68 @@
                 for step_y in range(ord_y):
                     index = ord_at(step_y, step_z)
                     tile = recv_buf[index]
+                    energies = energies + tile
                     for col in range(columns):
                         sums[col % 4] = sums[col % 4] + harm[index, col] * tile[:, col : col + 1]
-        return (sums[0] + sums[1]) + (sums[2] + sums[3])
+        return (sums[0] + sums[1]) + (sums[2] + sums[3]), energies[0:1, CURVE_COLUMN : CURVE_COLUMN + 1]
 
     leg_copy.wait()
     done, recv_buf = per_cycle(windows_ref[pl.ds(2 * CYCLES_HERE, CYCLES_HERE), :], jnp.zeros((1, 1), jnp.float32))
 
     ids_done = gather_ord(ids_send, ids_recv)
-    ids_done.wait_recv()
-    ids_copy = pltpu.make_async_copy(ids_recv, ids_smem, local_sem.at[2])
-    ids_copy.start()
-    ids_copy.wait()
-    first_order = ord_here * block
-
-    def find(owner, found):
-        found = list(found)
-        for slot in range(block):
-            number = ids_smem[owner, 0, slot]
-            for order in range(block):
-                found[order] = jnp.where(number == first_order + order, owner * block + slot, found[order])
-        return tuple(found)
-
-    found = lax.fori_loop(0, ords, find, tuple(jnp.int32(0) for unused in range(block)))
-    for order in range(block):
-        slot_smem[order] = found[order]
     inv_copy.wait()
-
+    build_spread()
+    third = (ords - 1) // 3
+    send_spread(0, third)
     done.wait_recv()
     summed, unused = adjoint(recv_buf, rows_ref[0])
-    residual = exchange_ord(summed, own_ref)
-    residual = jnp.where(inside, residual, 0.0)
-    precond = precondition(residual)
+    residual = jnp.where(inside, summed, 0.0)
+    sent = send_ord(residual)
+    send_spread(third, 2 * third)
+    find_slots()
+    owned = jnp.where(inside, take_ord(sent, own_ref), 0.0)
+    precond = precondition(owned, owner_table, live)
+    sent = send_ord(with_energy(owned, precond))
+    send_spread(2 * third, ords - 1)
+    chosen = take_ord(sent, slot_smem)
+    lines, energy_now = exchange_obs(chosen)
+    direction = jnp.where(inside, chosen, 0.0)
     solution = jnp.zeros((8, LANES), jnp.float32)
-    direction = None
-    coefficients = None
-    energy_now = None
+    gradient = None
+    nothing = jnp.zeros((1, 1), jnp.float32)
     for iteration in range(ITERS):
-        chosen = exchange_ord(with_energy(residual, precond), slot_smem)
-        lines, energy = exchange_obs(chosen)
         if iteration == 0:
-            direction, coefficients = precond, lines
+
+            def prepare():
+                build_inv()
+                send_inv(0, third)
+
+            gradient, unused = synthesize(lines, nothing, rows_ref[1], prepare)
         else:
+            precond = precondition(residual, lambda slot: inv_block[slot], live_block)
+            lines, energy_block = exchange_obs(with_energy(residual, precond))
+            ahead, energy = synthesize(lines, energy_block, rows_ref[1], lambda: None)
             ratio = energy / energy_now
+            gradient = ahead + ratio * gradient
             direction = precond + ratio * direction
-            coefficients = lines + ratio * coefficients
-        energy_now = energy
-        gradient = synthesize(coefficients, rows_ref[1])
+            energy_now = energy
         weighted = windows_ref[pl.ds(CYCLES_HERE, CYCLES_HERE), :] * gradient
         curve = jnp.sum(jnp.sum(weighted * gradient, axis=1, keepdims=True), axis=0, keepdims=True)
         done, recv_buf = per_cycle(weighted, curve)
+        if iteration == 0:
+            send_inv(third, ords - 1)
         done.wait_recv()
         summed, curvature = adjoint(recv_buf, rows_ref[0])
         step_size = energy_now / curvature
         solution = solution + step_size * direction
-        if iteration + 1 == ITERS:
-            sent_solution = send_obs(solution)
-        image = jnp.where(inside, exchange_ord(summed, own_ref), 0.0)
-        residual = residual - step_size * image
-        if iteration + 1 < ITERS:
-            precond = precondition(residual)
-
-    sent = [(sent_solution, solution_ref), (send_obs(residual), residual_ref)]
+        residual = residual - step_size * jnp.where(inside, summed, 0.0)
+        if iteration == 0:
+            take_inv()
+
+    sent_solution, sent_residual = send_ord(solution), send_ord(residual)
+    sent_solution = send_obs(take_ord(sent_solution, own_ref))
+    sent_residual = send_obs(take_ord(sent_residual, own_ref))
+    sent = [(sent_solution, solution_ref), (sent_residual, residual_ref)]
     for exchange, out in sent:
         lines, unused = take_obs(exchange)
         column[pl.ds(0, degrees), :] = lines
@@ -476,9 +569,10 @@
     dims = (block, degrees, cycles, ord_y, ord_z, obs_x)
     column_rows = -(-max(degrees, 1) // LANES) * LANES
     tile_rounds = 1 + 2 * ITERS
-    share_rounds = 1 + 2 * ITERS
+    share_rounds = 4
     all_rounds = 2 * ITERS + 2
-    total_rounds = 1 + tile_rounds + (1 + ITERS) + share_rounds + all_rounds + ITERS * (ord_z // 2)
+    deep = -(-(column_rows // LANES * GROUPS * 2) // ords)
+    total_rounds = 1 + tile_rounds + (1 + ITERS) + share_rounds + all_rounds + ITERS * (ord_z // 2) + 2
     scratch = [
         pltpu.VMEM((ords, 2 * block, CYCLES_HERE, SLOTS), jnp.float32),
         pltpu.VMEM((block, degrees, cycles), jnp.float32),
@@ -496,8 +590,15 @@
         pltpu.VMEM((1, LANES), jnp.int32),
         pltpu.VMEM((ords, 1, LANES), jnp.int32),
         pltpu.SMEM((ords, 1, LANES), jnp.int32),
+        pltpu.VMEM((8, LANES), jnp.int32),
+        pltpu.SMEM((8, LANES), jnp.int32),
         pltpu.SMEM((block,), jnp.int32),
-        pltpu.SemaphoreType.DMA((3,)),
+        pltpu.VMEM((ords, block, deep, 4, LANES), jnp.float32),
+        pltpu.VMEM((ords * block, deep, 4, LANES), jnp.float32),
+        pltpu.VMEM((ords, block, deep, 4, LANES), jnp.float32),
+        pltpu.VMEM((ords, block, deep, 4, LANES), jnp.float32),
+        pltpu.VMEM((block, SHARE, column_rows), jnp.float32),
+        pltpu.SemaphoreType.DMA((4,)),
         pltpu.SemaphoreType.DMA((total_rounds,)),
         pltpu.SemaphoreType.DMA((total_rounds,)),
     ]

time: 128 us -> 118 us (0.922)
  Pallas kernels: 124 us -> 113 us
    pallas_call x1, Pallas kernels: 122 us -> 111 us  [body(): pl.pallas_call(functools.partial(main_kernel, dims), out_shape=(result, r...]
where the time goes in v3:
time: 118 us; the launch traced here: 117 us
  Pallas kernels  113 us (96%)
  local copies, waits for them, and re-layouts  2.72 us (2%)
  between operations  1.29 us (1%)
    pallas_call x1, Pallas kernels, body(): pl.pallas_call(functools.partial(main_kernel, dims), out_shape=(result, r...  111 us
    unnamed x2, local copies, waits for them, and re-layouts  2.72 us

profile of v3, /device:TPU:1, one launch (start us, length us, event | category | flops | bytes accessed | tf_op | source)
XLA Modules:
  0.0 117.5 jit_solution(10904211535868989819)
XLA Ops:
  1.3 2.1 %windows.1.windows_ref = f32[24,256]{1,0:T(8,128)} custom-call(s32[1]{0:T(128)S(6)} %copy.12.count_ref, s32[256,128]{1,0:T(8,128)} %bitcast.6, f32[256,128]{1,0:T(8,128)} %bitcast.7, f32[256,128]{1,0:T(8,128)} %bitcast.8, f32[256,128]{1,0:T(8,128)} %bitcast.9), custom_call_target="tpu_custom_call" | custom-call | tf_op jit(solution)/shard_map/windows/pallas_call | solution.py:561
  3.3 111.4 %solve.1 = (f32[9,2,288]{2,1,0:T(2,128)}, f32[9,2,288]{2,1,0:T(2,128)}) custom-call(s32[9]{0:T(128)} %own_ref.1, f32[24,256]{1,0:T(8,128)} %windows.1.windows_ref, f32[9,288,256]{2,1,0:T(8,128)} %bitcast.5, f32[9,288,288]{2,1,0:T(8,128)} %inv_hbm.1), custom_call_target="tpu_custom_call" | custom-call | tf_op jit(solution)/shard_map/solve/pallas_call | solution.py:605
  114.7 1.4 %copy.13 = f32[9,2,288]{2,1,0:T(2,128)} copy(f32[9,2,288]{2,1,0:T(2,128)} %get-tuple-element.4) | data formatting | bytes 41472
  116.1 1.4 %copy.14 = f32[9,2,288]{2,1,0:T(2,128)} copy(f32[9,2,288]{2,1,0:T(2,128)} %get-tuple-element.5) | data formatting | bytes 41472

commit v4 on v3

--- a/solution.py
+++ b/solution.py
@@ -75,12 +75,32 @@
                 out_ref[pl.ds(which * CYCLES_HERE + step, 1), cut] = value
 
 
+def unpacked(shares, degrees):
+    pieces = []
+    for owner in range(shares.shape[0]):
+        for piece in range(GROUPS):
+            if owner * SHARE + piece * 8 < degrees:
+                lines = shares[owner]
+                pieces.append(pltpu.roll(lines, LANES - GROUP * piece, 1) if piece else lines)
+    return jnp.concatenate(pieces, axis=0)
+
+
+def finish_kernel(packed_ref, solution_ref, residual_ref, column):
+    block, unused, degrees = solution_ref.shape
+    column[...] = jnp.zeros(column.shape, jnp.float32)
+    for which, out in enumerate((solution_ref, residual_ref)):
+        column[pl.ds(0, degrees), :] = unpacked(packed_ref.at[which], degrees)
+        by_slot = jnp.transpose(column[...])
+        for slot in range(block):
+            out[slot] = by_slot[2 * slot : 2 * slot + 2, :degrees]
+
+
 def offset(index):
     return ((index + 1) // 2) * (1 - 2 * (index % 2))
 
 
 def main_kernel(
-    dims, own_ref, windows_ref, leg_hbm, inv_hbm, solution_ref, residual_ref,
+    dims, own_ref, windows_ref, leg_hbm, inv_hbm, packed_ref,
     harm, leg, inv, column, rows_ref, tile_send, tile_recv, part_send, part_recv, share_send, share_recv,
     all_send, all_recv, ids_send, ids_recv, ids_smem, slot_vmem, slot_all, slot_smem, spread_send, spread_recv,
     inv_send, inv_recv, inv_block, local_sem, send_sem, recv_sem,
@@ -108,6 +128,9 @@
 
     def ord_peer(index):
         return ord_at(ord_y // 2 + offset(index % ord_y), ord_z // 2 + offset(index // ord_y))
+
+    def bulk_peer(index):
+        return ord_at(ord_y // 2 + offset(index // ord_z), ord_z // 2 + offset(index % ord_z))
 
     def obs_peer(index):
         step_x = obs_x // 2 + offset(index // 2)
@@ -245,7 +268,7 @@
         waits.append(done)
         return done, recv_buf
 
-    def adjoint(recv_buf, rows):
+    def adjoint(recv_buf, rows, meanwhile):
         per_order = jnp.transpose(recv_buf[...].reshape(cycles, LANES)[:, :32])
         rows[...] = per_order
         curve = jnp.sum(rows[pl.ds(CURVE_COLUMN, 1), :], axis=1, keepdims=True)
@@ -280,6 +303,7 @@
         recv_obs[obs_here] = send_buf[obs_here]
         done = whole(obs_copy, recv_obs, sems, obss - 1, obs_peer(0))
         waits.append(done)
+        meanwhile()
         done.wait_recv()
         summed = jnp.sum(recv_obs[...], axis=0)
         return summed, summed[0:1, SCALAR_LANE : SCALAR_LANE + 1]
@@ -318,19 +342,15 @@
         done, recv_buf = sent
         done.wait_recv()
         total = jnp.sum(recv_buf[...], axis=0)[0:1, SCALAR_LANE : SCALAR_LANE + 1]
-        pieces = []
-        for owner in range(obss):
-            for piece in range(GROUPS):
-                if owner * SHARE + piece * 8 < degrees:
-                    lines = recv_buf[owner]
-                    pieces.append(pltpu.roll(lines, LANES - GROUP * piece, 1) if piece else lines)
-        return jnp.concatenate(pieces, axis=0), total
+        return unpacked(recv_buf, degrees), total
 
     def exchange_obs(packed):
         return take_obs(send_obs(packed))
 
-    def precondition(packed, table_of, alive):
-        lines, unused = exchange_obs(packed)
+    def precondition(packed, table_of, alive, meanwhile):
+        sent = send_obs(packed)
+        meanwhile()
+        lines, unused = take_obs(sent)
         column[pl.ds(0, degrees), :] = lines
         by_slot = jnp.transpose(column[...])
         result = jnp.zeros((8, LANES), jnp.float32)
@@ -366,7 +386,7 @@
 
     def send_spread(first, last):
         def send(index, carry):
-            peer = ord_peer(index)
+            peer = bulk_peer(index)
             ord_copy(spread_send.at[peer], spread_recv.at[pl.ds(ord_here * block, block)], spread_sems, peer).start()
             return carry
 
@@ -389,7 +409,7 @@
 
     def send_inv(first, last):
         def send(index, carry):
-            peer = ord_peer(index)
+            peer = bulk_peer(index)
             ord_copy(inv_send.at[peer], inv_recv.at[ord_here], inv_sems, peer).start()
             return carry
 
@@ -484,20 +504,21 @@
     ids_done = gather_ord(ids_send, ids_recv)
     inv_copy.wait()
     build_spread()
-    third = (ords - 1) // 3
-    send_spread(0, third)
+    part = ords // 4
+    last_bulk = 3 * part
+    send_spread(0, part)
     done.wait_recv()
-    summed, unused = adjoint(recv_buf, rows_ref[0])
+    summed, unused = adjoint(recv_buf, rows_ref[0], lambda: send_spread(part, 2 * part))
     residual = jnp.where(inside, summed, 0.0)
     sent = send_ord(residual)
-    send_spread(third, 2 * third)
     find_slots()
     owned = jnp.where(inside, take_ord(sent, own_ref), 0.0)
-    precond = precondition(owned, owner_table, live)
+    precond = precondition(owned, owner_table, live, lambda: send_spread(2 * part, last_bulk))
     sent = send_ord(with_energy(owned, precond))
-    send_spread(2 * third, ords - 1)
     chosen = take_ord(sent, slot_smem)
-    lines, energy_now = exchange_obs(chosen)
+    sent = send_obs(chosen)
+    send_spread(last_bulk, ords - 1)
+    lines, energy_now = take_obs(sent)
     direction = jnp.where(inside, chosen, 0.0)
     solution = jnp.zeros((8, LANES), jnp.float32)
     gradient = None
@@ -507,11 +528,11 @@
 
             def prepare():
                 build_inv()
-                send_inv(0, third)
+                send_inv(0, part)
 
             gradient, unused = synthesize(lines, nothing, rows_ref[1], prepare)
         else:
-            precond = precondition(residual, lambda slot: inv_block[slot], live_block)
+            precond = precondition(residual, lambda slot: inv_block[slot], live_block, take_inv)
             lines, energy_block = exchange_obs(with_energy(residual, precond))
             ahead, energy = synthesize(lines, energy_block, rows_ref[1], lambda: None)
             ratio = energy / energy_now
@@ -522,25 +543,21 @@
         curve = jnp.sum(jnp.sum(weighted * gradient, axis=1, keepdims=True), axis=0, keepdims=True)
         done, recv_buf = per_cycle(weighted, curve)
         if iteration == 0:
-            send_inv(third, ords - 1)
+            send_inv(part, last_bulk)
         done.wait_recv()
-        summed, curvature = adjoint(recv_buf, rows_ref[0])
+        summed, curvature = adjoint(
+            recv_buf, rows_ref[0], (lambda: send_inv(last_bulk, ords - 1)) if iteration == 0 else (lambda: None)
+        )
         step_size = energy_now / curvature
         solution = solution + step_size * direction
         residual = residual - step_size * jnp.where(inside, summed, 0.0)
-        if iteration == 0:
-            take_inv()
 
     sent_solution, sent_residual = send_ord(solution), send_ord(residual)
     sent_solution = send_obs(take_ord(sent_solution, own_ref))
     sent_residual = send_obs(take_ord(sent_residual, own_ref))
-    sent = [(sent_solution, solution_ref), (sent_residual, residual_ref)]
-    for exchange, out in sent:
-        lines, unused = take_obs(exchange)
-        column[pl.ds(0, degrees), :] = lines
-        by_slot = jnp.transpose(column[...])
-        for slot in range(block):
-            out[slot] = by_slot[2 * slot : 2 * slot + 2, :degrees]
+    for which, (done, recv_buf) in enumerate((sent_solution, sent_residual)):
+        done.wait_recv()
+        packed_ref[which] = recv_buf[...]
     for done in waits:
         done.wait_send()
 
@@ -602,17 +619,25 @@
         pltpu.SemaphoreType.DMA((total_rounds,)),
         pltpu.SemaphoreType.DMA((total_rounds,)),
     ]
-    return pl.pallas_call(
+    packed = pl.pallas_call(
         functools.partial(main_kernel, dims),
-        out_shape=(result, result),
+        out_shape=jax.ShapeDtypeStruct((2, obss, 8, LANES), jnp.float32),
         in_specs=[smem, vmem, hbm, hbm],
-        out_specs=(vmem, vmem),
+        out_specs=vmem,
         scratch_shapes=scratch,
         compiler_params=pltpu.CompilerParams(
             collective_id=0, has_side_effects=True
         ),
         name="solve",
     )(order_of_slot, windows, legendre[0], precond_inv)
+    return pl.pallas_call(
+        finish_kernel,
+        out_shape=(result, result),
+        in_specs=[vmem],
+        out_specs=(vmem, vmem),
+        scratch_shapes=[pltpu.VMEM((column_rows, LANES), jnp.float32)],
+        name="unpack",
+    )(packed)
 
 
 def solution(mesh):

time: 118 us -> 112 us (0.949)
  local copies, waits for them, and re-layouts: 2.72 us -> 0 us
  Pallas kernels: 113 us -> 111 us
    pallas_call x1 -> x2, Pallas kernels: 111 us -> 109 us  [the longest x1 107 us: body(): pl.pallas_call(functools.partial(main_kernel, dims), out_shape=jax.ShapeD...]
    unnamed x2 -> x0, local copies, waits for them, and re-layouts: 2.72 us -> none
where the time goes in v4:
time: 112 us
  Pallas kernels  111 us (99%)
  between operations  1.28 us (1%)
    pallas_call x1, Pallas kernels, body(): pl.pallas_call(functools.partial(main_kernel, dims), out_shape=jax.ShapeD...  107 us

profile of v4, /device:TPU:1, one launch (start us, length us, event | category | flops | bytes accessed | tf_op | source)
XLA Modules:
  0.0 112.0 jit_solution(11067999655287192364)
XLA Ops:
  1.3 2.1 %windows.1.windows_ref = f32[24,256]{1,0:T(8,128)} custom-call(s32[1]{0:T(128)S(6)} %copy.10.count_ref, s32[256,128]{1,0:T(8,128)} %bitcast.6, f32[256,128]{1,0:T(8,128)} %bitcast.7, f32[256,128]{1,0:T(8,128)} %bitcast.8, f32[256,128]{1,0:T(8,128)} %bitcast.9), custom_call_target="tpu_custom_call" | custom-call | tf_op jit(solution)/shard_map/windows/pallas_call | solution.py:578
  3.3 107.0 %solve.1.packed_ref = f32[2,8,8,128]{3,2,1,0:T(8,128)} custom-call(s32[9]{0:T(128)} %own_ref.1, f32[24,256]{1,0:T(8,128)} %windows.1.windows_ref, f32[9,288,256]{2,1,0:T(8,128)} %bitcast.5, f32[9,288,288]{2,1,0:T(8,128)} %inv_hbm.1), custom_call_target="tpu_custom_call" | custom-call | tf_op jit(solution)/shard_map/solve/pallas_call | solution.py:622
  110.3 1.7 %unpack.1 = (f32[9,2,288]{2,1,0:T(2,128)}, f32[9,2,288]{2,1,0:T(2,128)}) custom-call(f32[2,8,8,128]{3,2,1,0:T(8,128)} %solve.1.packed_ref), custom_call_target="tpu_custom_call" | custom-call | tf_op jit(solution)/shard_map/unpack/pallas_call | solution.py:633

commit v5 on v4

--- a/solution.py
+++ b/solution.py
@@ -44,19 +44,20 @@
     return sine_out, cosine_out
 
 
-def prologue_kernel(total_obs, count_ref, cycle_ref, lon_ref, obs_ref, weight_ref, out_ref):
-    first_cycle = lax.axis_index("ord") * CYCLES_HERE
+def prologue_kernel(total_obs, quarter, count_ref, cycle_ref, lon_ref, obs_ref, weight_ref, out_ref):
+    first_cycle = lax.axis_index("ord") * 2
     rows = cycle_ref.shape[0]
     ids = cycle_ref[...]
-    starts = []
-    for step in range(CYCLES_HERE + 1):
-        below = jnp.where(ids < first_cycle + step, 1.0, 0.0)
-        starts.append(jnp.sum(below).astype(jnp.int32))
+
+    def before(cycle):
+        return jnp.sum(jnp.where(ids < cycle, 1.0, 0.0)).astype(jnp.int32)
+
+    starts = [[before(first_cycle + part * quarter + step) for step in range(3)] for part in range(4)]
     lane = lax.broadcasted_iota(jnp.int32, (1, LANES), 1)
     used = count_ref[0]
     for step in range(CYCLES_HERE):
-        start = starts[step]
-        count = starts[step + 1] - start
+        start = starts[step % 4][step // 4]
+        count = starts[step % 4][step // 4 + 1] - start
         row = start // LANES
         shift = start - row * LANES
         turn = lax.rem(LANES - shift, LANES)
@@ -101,9 +102,9 @@
 
 def main_kernel(
     dims, own_ref, windows_ref, leg_hbm, inv_hbm, packed_ref,
-    harm, leg, inv, column, rows_ref, tile_send, tile_recv, part_send, part_recv, share_send, share_recv,
+    harm, leg, inv, column, stage, rows_ref, tile_send, tile_recv, part_send, part_recv, share_send, share_recv,
     all_send, all_recv, ids_send, ids_recv, ids_smem, slot_vmem, slot_all, slot_smem, spread_send, spread_recv,
-    inv_send, inv_recv, inv_block, local_sem, send_sem, recv_sem,
+    inv_send, inv_recv, inv_block, last_send, last_recv, last_share, last_all, local_sem, send_sem, recv_sem,
 ):
     block, degrees, cycles, ord_y, ord_z, obs_x = dims
     ords = ord_y * ord_z
@@ -146,6 +147,7 @@
 
     lane = lax.broadcasted_iota(jnp.int32, (8, LANES), 1)
     sublane = lax.broadcasted_iota(jnp.int32, (8, LANES), 0)
+    place = lane - 32 * (sublane % 4)
     group = lane // GROUP
     inner = lane % GROUP
     slot_lane = inner // 2
@@ -237,7 +239,7 @@
         tiles[0] += 1
         sems = next_round()
         send_buf, recv_buf = tile_send[which], tile_recv[which]
-        corner = jnp.logical_and(lane == CURVE_COLUMN, sublane == 0)
+        corner = jnp.logical_and(place == CURVE_COLUMN, sublane == 0)
         empty = jnp.where(corner, curve, 0.0)
 
         def step(outer, carry):
@@ -249,7 +251,10 @@
                 tile = empty
                 for col in range(columns):
                     total = jnp.sum(harm[peer, col] * weighted, axis=1, keepdims=True)
-                    tile = jnp.where(lane == col, total, tile)
+                    tile = jnp.where(place == col, total, tile)
+                tile = jnp.concatenate(
+                    [jnp.sum(tile[4 * half : 4 * half + 4], axis=0, keepdims=True) for half in range(2)], axis=0
+                )
                 send_buf[peer] = tile
                 if inner_step < unroll - 1:
                     ord_copy(send_buf.at[peer], recv_buf.at[ord_here], sems, peer).start()
@@ -269,8 +274,10 @@
         return done, recv_buf
 
     def adjoint(recv_buf, rows, meanwhile):
-        per_order = jnp.transpose(recv_buf[...].reshape(cycles, LANES)[:, :32])
-        rows[...] = per_order
+        for source in range(ords):
+            stage[pl.ds(2 * source, 2), :] = recv_buf[source]
+        turned = jnp.transpose(stage[...])
+        rows[...] = jnp.concatenate([turned[32 * part : 32 * part + 32] for part in range(4)], axis=1)
         curve = jnp.sum(rows[pl.ds(CURVE_COLUMN, 1), :], axis=1, keepdims=True)
         lane_all = lax.broadcasted_iota(jnp.int32, (degrees, LANES), 1)
         total = jnp.zeros((degrees, LANES), jnp.float32)
@@ -316,19 +323,20 @@
         recv_buf[ord_here] = packed
         return gather_ord(send_buf, recv_buf), recv_buf
 
+    def choose(block_line, index_ref, chosen):
+        for slot in range(block):
+            number = index_ref[slot]
+            source = lax.div(number, block)
+            shift = lax.rem(2 * slot - 2 * (number - source * block) + LANES, LANES)
+            lines = pltpu.roll(block_line(source), shift, 1)
+            chosen = jnp.where(jnp.logical_and(inside, slot_lane == slot), lines, chosen)
+        return chosen
+
     def take_ord(sent, index_ref):
         done, recv_buf = sent
         done.wait_recv()
         everyone = jnp.sum(recv_buf[...], axis=0)
-        chosen = jnp.where(lane == SCALAR_LANE, everyone, 0.0)
-        for slot in range(block):
-            number = index_ref[slot]
-            source = lax.div(number, block)
-            place = number - source * block
-            turn = lax.rem(2 * slot - 2 * place + LANES, LANES)
-            lines = pltpu.roll(recv_buf[source], turn, 1)
-            chosen = jnp.where(jnp.logical_and(inside, slot_lane == slot), lines, chosen)
-        return chosen
+        return choose(lambda source: recv_buf[source], index_ref, jnp.where(lane == SCALAR_LANE, everyone, 0.0))
 
     def send_obs(packed):
         which = alls[0]
@@ -464,8 +472,13 @@
                 col = 2 * order + part
                 rows[pl.ds(col, 1), :] = jnp.sum(table * coefficients[:, col : col + 1], axis=0, keepdims=True)
         rows[pl.ds(CURVE_COLUMN, 1), :] = jnp.broadcast_to(energy, (1, cycles))
-        turned = jnp.transpose(rows[...]).reshape(ords, CYCLES_HERE, 32)
-        send_buf[:, :, pl.ds(0, 32)] = turned
+        quarter = cycles // 4
+        lines = rows[...]
+        turned = jnp.transpose(
+            jnp.concatenate([lines[:, part * quarter : part * quarter + quarter] for part in range(4)], axis=0)
+        )
+        for target in range(ords):
+            send_buf[target] = turned[2 * target : 2 * target + 2]
         recv_buf[ord_here] = send_buf[ord_here]
 
         half = ord_z // 2
@@ -492,7 +505,13 @@
             for step_z in steps:
                 for step_y in range(ord_y):
                     index = ord_at(step_y, step_z)
-                    tile = recv_buf[index]
+                    pair = recv_buf[index]
+                    tile = jnp.concatenate(
+                        [jnp.broadcast_to(pair[half : half + 1], (4, LANES)) for half in range(2)], axis=0
+                    )
+                    spread = tile
+                    for part in range(1, 4):
+                        tile = jnp.where(sublane % 4 == part, pltpu.roll(spread, LANES - 32 * part, 1), tile)
                     energies = energies + tile
                     for col in range(columns):
                         sums[col % 4] = sums[col % 4] + harm[index, col] * tile[:, col : col + 1]
@@ -552,12 +571,17 @@
         solution = solution + step_size * direction
         residual = residual - step_size * jnp.where(inside, summed, 0.0)
 
-    sent_solution, sent_residual = send_ord(solution), send_ord(residual)
-    sent_solution = send_obs(take_ord(sent_solution, own_ref))
-    sent_residual = send_obs(take_ord(sent_residual, own_ref))
-    for which, (done, recv_buf) in enumerate((sent_solution, sent_residual)):
-        done.wait_recv()
-        packed_ref[which] = recv_buf[...]
+    for which, value in enumerate((solution, residual)):
+        last_send[which] = value
+        last_recv[ord_here, which] = value
+    gather_ord(last_send, last_recv).wait_recv()
+    for which in range(2):
+        value = choose(lambda source, which=which: last_recv[source, which], own_ref, jnp.zeros((8, LANES), jnp.float32))
+        last_share[which] = value
+        last_all[obs_here, which] = value
+    gather_obs(last_share, last_all).wait_recv()
+    for which in range(2):
+        packed_ref[which] = last_all[:, which]
     for done in waits:
         done.wait_send()
 
@@ -576,7 +600,7 @@
     window = jax.ShapeDtypeStruct((3 * CYCLES_HERE, SLOTS), jnp.float32)
     lines = (slab // LANES, LANES)
     windows = pl.pallas_call(
-        functools.partial(prologue_kernel, float(slab * obss)),
+        functools.partial(prologue_kernel, float(slab * obss), cycles // 4),
         out_shape=window,
         in_specs=[smem, vmem, vmem, vmem, vmem],
         out_specs=vmem,
@@ -586,18 +610,19 @@
     dims = (block, degrees, cycles, ord_y, ord_z, obs_x)
     column_rows = -(-max(degrees, 1) // LANES) * LANES
     tile_rounds = 1 + 2 * ITERS
-    share_rounds = 4
-    all_rounds = 2 * ITERS + 2
+    share_rounds = 2
+    all_rounds = 2 * ITERS
     deep = -(-(column_rows // LANES * GROUPS * 2) // ords)
-    total_rounds = 1 + tile_rounds + (1 + ITERS) + share_rounds + all_rounds + ITERS * (ord_z // 2) + 2
+    total_rounds = 1 + tile_rounds + (1 + ITERS) + share_rounds + all_rounds + ITERS * (ord_z // 2) + 4
     scratch = [
         pltpu.VMEM((ords, 2 * block, CYCLES_HERE, SLOTS), jnp.float32),
         pltpu.VMEM((block, degrees, cycles), jnp.float32),
         pltpu.VMEM((block, SHARE * obss, degrees), jnp.float32),
         pltpu.VMEM((column_rows, LANES), jnp.float32),
+        pltpu.VMEM((2 * ords, LANES), jnp.float32),
         [pltpu.VMEM((32, cycles), jnp.float32), pltpu.VMEM((32, cycles), jnp.float32)],
-        buffers(tile_rounds, ords, CYCLES_HERE, LANES),
-        buffers(tile_rounds, ords, CYCLES_HERE, LANES),
+        buffers(tile_rounds, ords, 2, LANES),
+        buffers(tile_rounds, ords, 2, LANES),
         buffers(1 + ITERS, obss, 8, LANES),
         buffers(1 + ITERS, obss, 8, LANES),
         buffers(share_rounds, 8, LANES),
@@ -615,6 +640,10 @@
         pltpu.VMEM((ords, block, deep, 4, LANES), jnp.float32),
         pltpu.VMEM((ords, block, deep, 4, LANES), jnp.float32),
         pltpu.VMEM((block, SHARE, column_rows), jnp.float32),
+        pltpu.VMEM((2, 8, LANES), jnp.float32),
+        pltpu.VMEM((ords, 2, 8, LANES), jnp.float32),
+        pltpu.VMEM((2, 8, LANES), jnp.float32),
+        pltpu.VMEM((obss, 2, 8, LANES), jnp.float32),
         pltpu.SemaphoreType.DMA((4,)),
         pltpu.SemaphoreType.DMA((total_rounds,)),
         pltpu.SemaphoreType.DMA((total_rounds,)),

time: 112 us -> 111 us (level)
  Pallas kernels: 111 us -> 109 us
    pallas_call x1, Pallas kernels: 107 us -> 106 us  [body(): pl.pallas_call(functools.partial(main_kernel, dims), out_shape=jax.ShapeD...]
where the time goes in v5:
time: 111 us
  Pallas kernels  109 us (98%)
  between operations  1.28 us (1%)
    pallas_call x1, Pallas kernels, body(): pl.pallas_call(functools.partial(main_kernel, dims), out_shape=jax.ShapeD...  106 us

profile of v5, /device:TPU:1, one launch (start us, length us, event | category | flops | bytes accessed | tf_op | source)
XLA Modules:
  0.0 110.7 jit_solution(11265305419319105251)
XLA Ops:
  1.3 2.1 %windows.1.windows_ref = f32[24,256]{1,0:T(8,128)} custom-call(s32[1]{0:T(128)S(6)} %copy.10.count_ref, s32[256,128]{1,0:T(8,128)} %bitcast.6, f32[256,128]{1,0:T(8,128)} %bitcast.7, f32[256,128]{1,0:T(8,128)} %bitcast.8, f32[256,128]{1,0:T(8,128)} %bitcast.9), custom_call_target="tpu_custom_call" | custom-call | tf_op jit(solution)/shard_map/windows/pallas_call | solution.py:602
  3.4 105.6 %solve.1.packed_ref = f32[2,8,8,128]{3,2,1,0:T(8,128)} custom-call(s32[9]{0:T(128)} %own_ref.1, f32[24,256]{1,0:T(8,128)} %windows.1.windows_ref, f32[9,288,256]{2,1,0:T(8,128)} %bitcast.5, f32[9,288,288]{2,1,0:T(8,128)} %inv_hbm.1), custom_call_target="tpu_custom_call" | custom-call | tf_op jit(solution)/shard_map/solve/pallas_call | solution.py:651
  109.0 1.7 %unpack.1 = (f32[9,2,288]{2,1,0:T(2,128)}, f32[9,2,288]{2,1,0:T(2,128)}) custom-call(f32[2,8,8,128]{3,2,1,0:T(8,128)} %solve.1.packed_ref), custom_call_target="tpu_custom_call" | custom-call | tf_op jit(solution)/shard_map/unpack/pallas_call | solution.py:662

commit v6 on v5

--- a/solution.py
+++ b/solution.py
@@ -44,13 +44,13 @@
     return sine_out, cosine_out
 
 
-def prologue_kernel(total_obs, quarter, count_ref, cycle_ref, lon_ref, obs_ref, weight_ref, out_ref):
+def fill_windows(total_obs, quarter, count_ref, cycle_ref, lon_ref, obs_ref, weight_ref, out_ref):
     first_cycle = lax.axis_index("ord") * 2
     rows = cycle_ref.shape[0]
     ids = cycle_ref[...]
 
     def before(cycle):
-        return jnp.sum(jnp.where(ids < cycle, 1.0, 0.0)).astype(jnp.int32)
+        return jnp.sum(jnp.where(ids < cycle, 1, 0))
 
     starts = [[before(first_cycle + part * quarter + step) for step in range(3)] for part in range(4)]
     lane = lax.broadcasted_iota(jnp.int32, (1, LANES), 1)
@@ -101,7 +101,7 @@
 
 
 def main_kernel(
-    dims, own_ref, windows_ref, leg_hbm, inv_hbm, packed_ref,
+    dims, total_obs, own_ref, count_ref, cycle_ref, lon_ref, obs_ref, weight_ref, leg_hbm, inv_hbm, packed_ref, windows_ref,
     harm, leg, inv, column, stage, rows_ref, tile_send, tile_recv, part_send, part_recv, share_send, share_recv,
     all_send, all_recv, ids_send, ids_recv, ids_smem, slot_vmem, slot_all, slot_smem, spread_send, spread_recv,
     inv_send, inv_recv, inv_block, last_send, last_recv, last_share, last_all, local_sem, send_sem, recv_sem,
@@ -169,6 +169,7 @@
         rows_ref[which][...] = jnp.zeros((32, cycles), jnp.float32)
     column[...] = jnp.zeros(column.shape, jnp.float32)
 
+    fill_windows(total_obs, cycles // 4, count_ref, cycle_ref, lon_ref, obs_ref, weight_ref, windows_ref)
     longitude = windows_ref[pl.ds(0, CYCLES_HERE), :]
 
     def harmonic_block(index, carry):
@@ -597,15 +598,7 @@
     vmem = pl.BlockSpec(memory_space=pltpu.VMEM)
     smem = pl.BlockSpec(memory_space=pltpu.SMEM)
     hbm = pl.BlockSpec(memory_space=pltpu.HBM)
-    window = jax.ShapeDtypeStruct((3 * CYCLES_HERE, SLOTS), jnp.float32)
     lines = (slab // LANES, LANES)
-    windows = pl.pallas_call(
-        functools.partial(prologue_kernel, float(slab * obss), cycles // 4),
-        out_shape=window,
-        in_specs=[smem, vmem, vmem, vmem, vmem],
-        out_specs=vmem,
-        name="windows",
-    )(obs_count, cycle_of.reshape(lines), longitude.reshape(lines), observed.reshape(lines), obs_weight.reshape(lines))
     result = jax.ShapeDtypeStruct((block, 2, degrees), jnp.float32)
     dims = (block, degrees, cycles, ord_y, ord_z, obs_x)
     column_rows = -(-max(degrees, 1) // LANES) * LANES
@@ -615,6 +608,7 @@
     deep = -(-(column_rows // LANES * GROUPS * 2) // ords)
     total_rounds = 1 + tile_rounds + (1 + ITERS) + share_rounds + all_rounds + ITERS * (ord_z // 2) + 4
     scratch = [
+        pltpu.VMEM((3 * CYCLES_HERE, SLOTS), jnp.float32),
         pltpu.VMEM((ords, 2 * block, CYCLES_HERE, SLOTS), jnp.float32),
         pltpu.VMEM((block, degrees, cycles), jnp.float32),
         pltpu.VMEM((block, SHARE * obss, degrees), jnp.float32),
@@ -649,16 +643,19 @@
         pltpu.SemaphoreType.DMA((total_rounds,)),
     ]
     packed = pl.pallas_call(
-        functools.partial(main_kernel, dims),
+        functools.partial(main_kernel, dims, float(slab * obss)),
         out_shape=jax.ShapeDtypeStruct((2, obss, 8, LANES), jnp.float32),
-        in_specs=[smem, vmem, hbm, hbm],
+        in_specs=[smem, smem, vmem, vmem, vmem, vmem, hbm, hbm],
         out_specs=vmem,
         scratch_shapes=scratch,
         compiler_params=pltpu.CompilerParams(
             collective_id=0, has_side_effects=True
         ),
         name="solve",
-    )(order_of_slot, windows, legendre[0], precond_inv)
+    )(
+        order_of_slot, obs_count, cycle_of.reshape(lines), longitude.reshape(lines), observed.reshape(lines),
+        obs_weight.reshape(lines), legendre[0], precond_inv,
+    )
     return pl.pallas_call(
         finish_kernel,
         out_shape=(result, result),

time: 111 us -> 109 us (0.982)
    pallas_call x2 -> x1, Pallas kernels: 108 us -> 106 us  [body(): pl.pallas_call(functools.partial(main_kernel, dims, float(slab * obss)),...]
where the time goes in v6:
time: 109 us
  Pallas kernels  108 us (99%)
  between operations  1.29 us (1%)
    pallas_call x1, Pallas kernels, body(): pl.pallas_call(functools.partial(main_kernel, dims, float(slab * obss)),...  106 us

profile of v6, /device:TPU:1, one launch (start us, length us, event | category | flops | bytes accessed | tf_op | source)
XLA Modules:
  0.0 109.2 jit_solution(2795736074721264364)
XLA Ops:
  1.3 106.2 %solve.1.packed_ref = f32[2,8,8,128]{3,2,1,0:T(8,128)} custom-call(s32[9]{0:T(128)} %own_ref.1, s32[1]{0:T(128)S(6)} %copy.10.count_ref, s32[256,128]{1,0:T(8,128)} %bitcast.6, f32[256,128]{1,0:T(8,128)} %bitcast.7, f32[256,128]{1,0:T(8,128)} %bitcast.8, f32[256,128]{1,0:T(8,128)} %bitcast.9, f32[9,288,256]{2,1,0:T(8,128)} %bitcast.5, f32[9,288,288]{2,1,0:T(8,128)} %inv_hbm.1), custom_call_target="tpu_custom_call" | custom-call | tf_op jit(solution)/shard_map/solve/pallas_call | solution.py:645
  107.5 1.7 %unpack.1 = (f32[9,2,288]{2,1,0:T(2,128)}, f32[9,2,288]{2,1,0:T(2,128)}) custom-call(f32[2,8,8,128]{3,2,1,0:T(8,128)} %solve.1.packed_ref), custom_call_target="tpu_custom_call" | custom-call | tf_op jit(solution)/shard_map/unpack/pallas_call | solution.py:659

commit v7 on v6

--- a/solution.py
+++ b/solution.py
@@ -110,7 +110,7 @@
     ords = ord_y * ord_z
     obss = obs_x * 2
     columns = 2 * block
-    unroll = 2 * ord_y
+    unroll = 4 * ord_y
     ord_here = lax.axis_index("ord")
     obs_here = lax.axis_index("obs")
 

time: 109 us -> 109 us (level)
  no operation moved by 1% of the time
where the time goes in v7:
time: 109 us
  Pallas kernels  108 us (99%)
  between operations  1.29 us (1%)
    pallas_call x1, Pallas kernels, body(): pl.pallas_call(functools.partial(main_kernel, dims, float(slab * obss)),...  106 us

profile of v7, /device:TPU:1, one launch (start us, length us, event | category | flops | bytes accessed | tf_op | source)
XLA Modules:
  0.0 109.3 jit_solution(16113498178934033631)
XLA Ops:
  1.3 106.3 %solve.1.packed_ref = f32[2,8,8,128]{3,2,1,0:T(8,128)} custom-call(s32[9]{0:T(128)} %own_ref.1, s32[1]{0:T(128)S(6)} %copy.10.count_ref, s32[256,128]{1,0:T(8,128)} %bitcast.6, f32[256,128]{1,0:T(8,128)} %bitcast.7, f32[256,128]{1,0:T(8,128)} %bitcast.8, f32[256,128]{1,0:T(8,128)} %bitcast.9, f32[9,288,256]{2,1,0:T(8,128)} %bitcast.5, f32[9,288,288]{2,1,0:T(8,128)} %inv_hbm.1), custom_call_target="tpu_custom_call" | custom-call | tf_op jit(solution)/shard_map/solve/pallas_call | solution.py:645
  107.6 1.7 %unpack.1 = (f32[9,2,288]{2,1,0:T(2,128)}, f32[9,2,288]{2,1,0:T(2,128)}) custom-call(f32[2,8,8,128]{3,2,1,0:T(8,128)} %solve.1.packed_ref), custom_call_target="tpu_custom_call" | custom-call | tf_op jit(solution)/shard_map/unpack/pallas_call | solution.py:659
